TPU v7x, 1024 devices: a whole 8x8x8 slice. The times are simulated.
1024 devices in a mesh: gz: 8 (over x), gy: 32 (over y_lo, z), gx: 4 (over y_hi, core).
Axes of the slice: x: 8, y: 8 (y_hi: 2, y_lo: 4; y = y_hi * 4 + y_lo), z: 8, core: 2. Of those that a mesh axis runs over, the one named last changes fastest.
Arguments:
- density: float32 [64, 256, 512], P('gz', 'gy', 'gx'), may hold values from 0.3 to 3
- velocity: float32 [3, 64, 256, 512], P(None, 'gz', 'gy', 'gx'), may hold values from -3 to 3
- pressure: float32 [64, 256, 512], P('gz', 'gy', 'gx'), may hold values from 0.3 to 3
- field: float32 [3, 64, 256, 512], P(None, 'gz', 'gy', 'gx'), may hold values from -3 to 3
- corona: int32 [64], replicated, may hold values from 0 to 1, as said below
Outputs:
- conserved: float32 [5, 64, 256, 512], P(None, 'gz', 'gy', 'gx')
- faces_new: float32 [3, 64, 256, 512], P(None, 'gz', 'gy', 'gx')
Inputs may be any that keep to these rules, and one draw needn't show every extreme that they name: `corona`: 1 marks a cooled slab; every slab farther from the midplane than a drawn height (one for each half of z) is cooled, and some other slabs are cooled too.
All inputs are finite; a program needn't handle non-finite values.
Results may differ from a plain program's by a relative error of at most 0.00002.
Values sent between devices are 32-bit elements; how exact they have to be, the bound alone decides.
No kernel may reach another device: no remote copies, remote signals or barrier semaphores. Data moves between devices by JAX's collectives and lax.ppermute only.
A program may use at most 32 MiB of HBM per device.

v0:
```python
import jax
import jax.numpy as jnp
from jax import lax
from jax.sharding import PartitionSpec as P

COOL_STEPS = 8


adiabatic = 5.0 / 3.0
courant = 0.08
cool_rate = 0.03
gravity = 1.0
cyclic_pairs = ((2, 1), (0, 2), (1, 0))


def with_halo(cells, sides, width, closed):
    for axis, dim in sides:
        count = lax.axis_size(axis)
        ends = count if closed else count - 1
        head = lax.slice_in_dim(cells, 0, width, axis=dim)
        tail = lax.slice_in_dim(cells, cells.shape[dim] - width, cells.shape[dim], axis=dim)
        cells = jnp.concatenate(
            [
                lax.ppermute(tail, axis, [(i, (i + 1) % count) for i in range(ends)]),
                cells,
                lax.ppermute(head, axis, [((i + 1) % count, i) for i in range(ends)]),
            ],
            axis=dim,
        )
    return cells


def shift_up(values, along):
    return jnp.roll(values, -1, along)


def shift_down(values, along):
    return jnp.roll(values, 1, along)


def cool_cells(density, pressure):
    for subcycle in range(COOL_STEPS):
        pressure = pressure / (1.0 + cool_rate * jnp.sqrt(density * pressure))
    return pressure


def cool_marked(density, pressure, marks):
    return jnp.where(marks[:, None, None] == 1, cool_cells(density, pressure), pressure)


def state_terms(density, velocity, pressure, magnetic, normal_axis):
    others = [component for component in range(3) if component != normal_axis]
    normal_field = magnetic[normal_axis]
    transverse = (
        magnetic[others[0]] * magnetic[others[0]] + magnetic[others[1]] * magnetic[others[1]]
    )
    squared = transverse + normal_field * normal_field
    total_pressure = pressure + 0.5 * squared
    kinetic = velocity[0] * velocity[0] + velocity[1] * velocity[1] + velocity[2] * velocity[2]
    alignment = velocity[0] * magnetic[0] + velocity[1] * magnetic[1] + velocity[2] * magnetic[2]
    energy = pressure / (adiabatic - 1.0) + 0.5 * density * kinetic + 0.5 * squared
    sound = adiabatic * pressure / density
    along_field = normal_field * normal_field / density
    across_field = transverse / density
    fast_speed = jnp.sqrt(
        0.5
        * (
            sound
            + along_field
            + across_field
            + jnp.sqrt((sound - along_field - across_field) ** 2 + 4.0 * sound * across_field)
        )
    )
    normal_speed = velocity[normal_axis]
    conserved = (
        [density]
        + [density * velocity[component] for component in range(3)]
        + [energy]
        + [magnetic[component] for component in others]
    )
    fluxes = [density * normal_speed]
    for component in range(3):
        moment = density * velocity[component] * normal_speed - magnetic[component] * normal_field
        if component == normal_axis:
            moment = moment + total_pressure
        fluxes.append(moment)
    fluxes.append((energy + total_pressure) * normal_speed - normal_field * alignment)
    for component in others:
        fluxes.append(normal_speed * magnetic[component] - velocity[component] * normal_field)
    return (normal_speed, fast_speed, conserved, fluxes)


def interface_flux(density, velocity, pressure, centre, normal_face, normal_axis):
    lower_field = [shift_down(member, normal_axis) for member in centre]
    lower_field[normal_axis] = normal_face
    upper_field = list(centre)
    upper_field[normal_axis] = normal_face
    lower_terms = state_terms(
        shift_down(density, normal_axis),
        [shift_down(member, normal_axis) for member in velocity],
        shift_down(pressure, normal_axis),
        lower_field,
        normal_axis,
    )
    upper_terms = state_terms(density, velocity, pressure, upper_field, normal_axis)
    slowest = jnp.minimum(
        jnp.minimum(lower_terms[0] - lower_terms[1], upper_terms[0] - upper_terms[1]), 0.0
    )
    fastest = jnp.maximum(
        jnp.maximum(lower_terms[0] + lower_terms[1], upper_terms[0] + upper_terms[1]), 0.0
    )
    inverse = 1.0 / (fastest - slowest)
    result = []
    for member in range(7):
        lower_flux = lower_terms[3][member]
        upper_flux = upper_terms[3][member]
        jump = upper_terms[2][member] - lower_terms[2][member]
        result.append(
            (fastest * lower_flux - slowest * upper_flux + slowest * fastest * jump) * inverse
        )
    return result


def advance(extended, height):
    density = extended[0]
    velocity = [extended[1], extended[2], extended[3]]
    pressure = extended[4]
    faces = [extended[5], extended[6], extended[7]]
    centre = [
        0.5 * (faces[component] + shift_up(faces[component], component)) for component in range(3)
    ]
    fluxes = [
        interface_flux(density, velocity, pressure, centre, faces[direction], direction)
        for direction in range(3)
    ]
    kinetic = velocity[0] * velocity[0] + velocity[1] * velocity[1] + velocity[2] * velocity[2]
    squared = centre[0] * centre[0] + centre[1] * centre[1] + centre[2] * centre[2]
    energy = pressure / (adiabatic - 1.0) + 0.5 * density * kinetic + 0.5 * squared
    conserved = [
        density,
        density * velocity[0],
        density * velocity[1],
        density * velocity[2],
        energy,
    ]
    inner = (slice(2, -2), slice(2, -2), slice(2, -2))
    updated = []
    for member in range(5):
        change = jnp.zeros_like(density)
        for direction in range(3):
            change = (
                change + shift_up(fluxes[direction][member], direction) - fluxes[direction][member]
            )
        updated.append((conserved[member] - courant * change)[inner])
    pull = -gravity * height[:, None, None]
    updated[1] = updated[1] + courant * density[inner] * pull
    updated[4] = updated[4] + courant * density[inner] * velocity[0][inner] * pull
    electric = []
    for edge in range(3):
        first, second = cyclic_pairs[edge]
        first_others = [component for component in range(3) if component != first]
        second_others = [component for component in range(3) if component != second]
        first_flux = fluxes[first][5 + first_others.index(second)]
        second_flux = fluxes[second][5 + second_others.index(first)]
        electric.append(
            0.25
            * (
                second_flux
                + shift_down(second_flux, first)
                - first_flux
                - shift_down(first_flux, second)
            )
        )
    new_faces = []
    for component in range(3):
        across, beyond = cyclic_pairs[component]
        curl = (
            shift_up(electric[beyond], across)
            - electric[beyond]
            - (shift_up(electric[across], beyond) - electric[across])
        )
        new_faces.append((faces[component] - courant * curl)[inner])
    return (jnp.stack(updated), jnp.stack(new_faces))


def clamp_dim(extended, dim, at_lower, at_upper):
    length = extended.shape[dim]
    lower_edge = lax.slice_in_dim(extended, 2, 3, axis=dim)
    upper_edge = lax.slice_in_dim(extended, length - 3, length - 2, axis=dim)
    lower_rims = jnp.where(
        at_lower,
        jnp.concatenate([lower_edge, lower_edge], dim),
        lax.slice_in_dim(extended, 0, 2, axis=dim),
    )
    upper_rims = jnp.where(
        at_upper,
        jnp.concatenate([upper_edge, upper_edge], dim),
        lax.slice_in_dim(extended, length - 2, length, axis=dim),
    )
    middle = lax.slice_in_dim(extended, 2, length - 2, axis=dim)
    return jnp.concatenate([lower_rims, middle, upper_rims], dim)


def rim_across_x(stacked):
    return with_halo(stacked, (("gx", 3),), 2, True)


def rim_across_yz(stacked):
    extended = with_halo(stacked, (("gz", 1), ("gy", 2)), 2, False)
    row_index = lax.axis_index("gy")
    extended = clamp_dim(extended, 2, row_index == 0, row_index == lax.axis_size("gy") - 1)
    slab_index = lax.axis_index("gz")
    return clamp_dim(extended, 1, slab_index == 0, slab_index == lax.axis_size("gz") - 1)


def on_device(density, velocity, pressure, field, corona):
    slabs = density.shape[0]
    slab_index = lax.axis_index("gz")
    marks = lax.dynamic_slice_in_dim(corona, slab_index * slabs, slabs)
    cooled = cool_marked(density, pressure, marks)
    stacked = jnp.concatenate([density[None], velocity, cooled[None], field], 0)
    extended = rim_across_x(rim_across_yz(stacked))
    total_slabs = slabs * lax.axis_size("gz")
    global_slab = slab_index * slabs + jnp.arange(slabs, dtype=jnp.int32)
    height = (2 * global_slab + 1 - total_slabs).astype(jnp.float32) / total_slabs
    return advance(extended, height)


def solution(mesh):
    return jax.shard_map(
        on_device,
        mesh=mesh,
        in_specs=(
            P("gz", "gy", "gx"),
            P(None, "gz", "gy", "gx"),
            P("gz", "gy", "gx"),
            P(None, "gz", "gy", "gx"),
            P(),
        ),
        out_specs=(P(None, "gz", "gy", "gx"), P(None, "gz", "gy", "gx")),
        check_vma=False,
    )
```

profile of v0, /device:TPU:22, one launch (start us, length us, event | category | flops | bytes accessed | tf_op | source)
XLA Modules:
  0.0 71.5 jit_solution(15456536235646153963)
XLA Ops:
  0.7 0.8 %dynamic-slice_compare_fusion = pred[8]{0:T(512)(128)(4,1)S(1)} fusion(s32[64]{0:T(128)} %param.9, s32[]{:T(128)S(6)} %select_n.37), kind=kLoop, calls=%fused_computation.239 | loop fusion | flops 8 | bytes 44 | tf_op jit(solution)/shard_map/eq | solution.py:48
  1.5 0.9 %fusion.21 = f32[1,8,8,128]{3,2,1,0:T(8,128)S(1)} fusion(f32[8,8,128]{2,1,0:T(8,128)} %param.7, f32[8,8,128]{2,1,0:T(8,128)} %param.5, pred[8]{0:T(512)(128)(4,1)S(1)} %dynamic-slice_compare_fusion), kind=kLoop, calls=%fused_computation.148 | loop fusion | flops 327680 | bytes 98312 | tf_op jit(solution)/shard_map/broadcast_in_dim | solution.py:221
  2.4 0.8 %pad_maximum_fusion.34 = (f32[8,2,8,128]{3,2,1,0:T(8,128)S(1)}, f32[8,2,8,128]{3,2,1,0:T(8,128)S(1)}) fusion(f32[3,8,8,128]{3,2,1,0:T(8,128)} %param.8, f32[1,8,8,128]{3,2,1,0:T(8,128)S(1)} %fusion.21, f32[3,8,8,128]{3,2,1,0:T(8,128)} %param.6, f32[1,8,8,128]{3,2,1,0:T(8,128)} %bitcast.335), kind=kLoop, calls=%fused_computation.144 | loop fusion | flops 98304 | bytes 393216 | tf_op jit(solution)/shard_map/slice | solution.py:21
  3.2 4.6 %collective-permute-start = (f32[8,2,8,128]{3,2,1,0:T(8,128)S(1)}, f32[8,2,8,128]{3,2,1,0:T(8,128)S(1)}, u32[]{:S(2)}, u32[]{:S(2)}) collective-permute-start(f32[8,2,8,128]{3,2,1,0:T(8,128)S(1)} %get-tuple-element.66), channel_id=1, source_target_pairs={{0,128},{128,256},{256,384},{384,512},{512,640},{640,768},{768,896... | collective-permute-start | bytes 196616 | tf_op jit(solution)/shard_map/ppermute | solution.py:24
  7.8 1.9 %collective-permute-start.1 = (f32[8,2,8,128]{3,2,1,0:T(8,128)S(1)}, f32[8,2,8,128]{3,2,1,0:T(8,128)S(1)}, u32[]{:S(2)}, u32[]{:S(2)}) collective-permute-start(f32[8,2,8,128]{3,2,1,0:T(8,128)S(1)} %get-tuple-element.67), channel_id=1, source_target_pairs={{128,0},{256,128},{384,256},{512,384},{640,512},{768,640},{896,768... | collective-permute-start | bytes 196616 | tf_op jit(solution)/shard_map/ppermute | solution.py:26
  9.8 5.4 %collective-permute-done.1 = f32[8,2,8,128]{3,2,1,0:T(8,128)S(1)} collective-permute-done((f32[8,2,8,128]{3,2,1,0:T(8,128)S(1)}, f32[8,2,8,128]{3,2,1,0:T(8,128)S(1)}, u32[]{:S(2)}, u32[]{:S(2)}) %collective-permute-start.1) | collective-permute-done | bytes 65568 | tf_op jit(solution)/shard_map/ppermute | solution.py:26
  15.2 1.1 %pad_maximum_fusion.29 = (f32[8,12,2,128]{3,2,1,0:T(2,128)S(1)}, f32[8,12,2,128]{3,2,1,0:T(2,128)S(1)}) fusion(f32[8,2,8,128]{3,2,1,0:T(8,128)S(1)} %collective-permute-done.1, f32[8,2,8,128]{3,2,1,0:T(8,128)S(1)} %collective-permute-done, f32[3,8,8,128]{3,2,1,0:T(8,128)} %param.8, f32[1,8,8,128]{3,2,1,0:T(8,128)S(1)} %fusion.21, ...), kind=kLoop, calls=%fused_computation.137 | loop fusion | flops 245760 | bytes 589824 | tf_op jit(solution)/shard_map/slice | solution.py:21
  16.3 5.2 %collective-permute-start.2 = (f32[8,12,2,128]{3,2,1,0:T(2,128)S(1)}, f32[8,12,2,128]{3,2,1,0:T(2,128)S(1)}, u32[]{:S(2)}, u32[]{:S(2)}) collective-permute-start(f32[8,12,2,128]{3,2,1,0:T(2,128)S(1)} %get-tuple-element.64), channel_id=1, source_target_pairs={{0,4},{4,8},{8,12},{12,16},{16,20},{20,24},{24,28},{28,32},{32,36}... | collective-permute-start | bytes 294920 | tf_op jit(solution)/shard_map/ppermute | solution.py:24
  21.5 13.8 %collective-permute-start.3 = (f32[8,12,2,128]{3,2,1,0:T(2,128)S(1)}, f32[8,12,2,128]{3,2,1,0:T(2,128)S(1)}, u32[]{:S(2)}, u32[]{:S(2)}) collective-permute-start(f32[8,12,2,128]{3,2,1,0:T(2,128)S(1)} %get-tuple-element.65), channel_id=1, source_target_pairs={{4,0},{8,4},{12,8},{16,12},{20,16},{24,20},{28,24},{32,28},{36,32}... | collective-permute-start | bytes 294920 | tf_op jit(solution)/shard_map/ppermute | solution.py:26
  35.3 1.1 %pad_maximum_fusion.36 = (f32[8,12,1,128]{3,2,1,0:T(1,128)S(1)}, f32[8,12,1,128]{3,2,1,0:T(1,128)S(1)}) fusion(f32[8,2,8,128]{3,2,1,0:T(8,128)S(1)} %collective-permute-done.1, f32[8,2,8,128]{3,2,1,0:T(8,128)S(1)} %collective-permute-done, f32[3,8,8,128]{3,2,1,0:T(8,128)} %param.8, f32[1,8,8,128]{3,2,1,0:T(8,128)S(1)} %fusion.21, ...), kind=kLoop, calls=%fused_computation.146 | loop fusion | flops 122880 | bytes 491520 | tf_op jit(solution)/shard_map/slice | solution.py:188
  36.6 1.0 %collective-permute-done.3 = f32[8,12,2,128]{3,2,1,0:T(2,128)S(1)} collective-permute-done((f32[8,12,2,128]{3,2,1,0:T(2,128)S(1)}, f32[8,12,2,128]{3,2,1,0:T(2,128)S(1)}, u32[]{:S(2)}, u32[]{:S(2)}) %collective-permute-start.3) | collective-permute-done | bytes 98336 | tf_op jit(solution)/shard_map/ppermute | solution.py:26
  38.3 0.7 copy.51
  38.9 0.7 copy.52
  39.6 5.3 %collective-permute-start.5 = (f32[8,12,12,2]{2,0,3,1:T(8,128)S(1)}, f32[8,12,12,2]{2,0,3,1:T(8,128)S(1)}, u32[]{:S(2)}, u32[]{:S(2)}) collective-permute-start(f32[8,12,12,2]{2,0,3,1:T(8,128)S(1)} %copy.52), channel_id=1, source_target_pairs={{1,0},{2,1},{3,2},{0,3},{5,4},{6,5},{7,6},{4,7},{9,8},{10,9},{11,1... | collective-permute-start | bytes 27656 | tf_op jit(solution)/shard_map/ppermute | solution.py:26
  45.0 2.1 %collective-permute-start.4 = (f32[8,12,12,2]{2,0,3,1:T(8,128)S(1)}, f32[8,12,12,2]{2,0,3,1:T(8,128)S(1)}, u32[]{:S(2)}, u32[]{:S(2)}) collective-permute-start(f32[8,12,12,2]{2,0,3,1:T(8,128)S(1)} %copy.51), channel_id=1, source_target_pairs={{0,1},{1,2},{2,3},{3,0},{4,5},{5,6},{6,7},{7,4},{8,9},{9,10},{10,1... | collective-permute-start | bytes 27656 | tf_op jit(solution)/shard_map/ppermute | solution.py:24
  47.1 8.8 %collective-permute-done.4 = f32[8,12,12,2]{2,0,3,1:T(8,128)S(1)} collective-permute-done((f32[8,12,12,2]{2,0,3,1:T(8,128)S(1)}, f32[8,12,12,2]{2,0,3,1:T(8,128)S(1)}, u32[]{:S(2)}, u32[]{:S(2)}) %collective-permute-start.4) | collective-permute-done | bytes 9248 | tf_op jit(solution)/shard_map/ppermute | solution.py:24
  55.9 0.7 copy.53
  56.6 0.7 copy.54
  57.5 0.7 pad_maximum_fusion
  59.4 0.6 add_multiply_fusion.3
  60.8 0.5 add_multiply_fusion.8
  62.0 0.8 %add_multiply_fusion.2 = (f32[12,12,132]{2,1,0:T(8,128)S(1)}, f32[12,12,132]{2,1,0:T(8,128)S(1)}, f32[12,12,132]{2,1,0:T(8,128)S(1)}) fusion(f32[12,12,132]{2,1,0:T(8,128)S(1)} %get-tuple-element.48, f32[12,11,132]{2,1,0:T(8,128)S(1)} %bitcast.315, f32[12,1,132]{2,1,0:T(1,128)S(1)} %slice.666, f32[12,11,132]{2,1,0:T(8,128)S(1)} %bitcast.288, ...), kind=kLoop, calls=%fused_computation.67 | loop fusion | flops 1235520 | bytes 1216512 | tf_op jit(solution)/shard_map/mul | solution.py:119
  62.8 0.4 add_multiply_fusion.15
  63.2 0.3 add_multiply_fusion.1
  63.6 0.6 add_multiply_fusion.7
  65.0 0.8 %add_multiply_fusion.5 = (f32[12,12,132]{2,1,0:T(8,128)S(1)}, f32[12,12,132]{2,1,0:T(8,128)S(1)}, f32[12,12,132]{2,1,0:T(8,128)S(1)}, f32[12,12,132]{2,1,0:T(8,1...) fusion(f32[12,12,132]{2,1,0:T(8,128)S(1)} %get-tuple-element.48, f32[12,12,131]{2,1,0:T(8,128)S(1)} %bitcast.318, ...), kind=kLoop, calls=%fused_computation.70 | loop fusion | flops 1235520 | bytes 1444608 | tf_op jit(solution)/shard_map/mul | solution.py:119
  65.8 0.4 add_multiply_fusion.9
  66.2 0.6 add_multiply_fusion.6
  66.8 0.4 add_multiply_fusion
  67.7 0.4 fusion.5
  69.5 0.6 pad_maximum_fusion.30
  70.9 0.7 copy-done.5
  (119 shorter events, 6.5 us)
Async XLA Ops:
  0.6 37.0 %copy-start.4 = (f32[8,8,128]{2,1,0:T(8,128)S(1)}, f32[8,8,128]{2,1,0:T(8,128)}, u32[]{:S(2)}) copy-start(f32[8,8,128]{2,1,0:T(8,128)} %param.5) | copy-start | bytes 98308
  0.6 37.0 %copy-start = (f32[3,8,8,128]{3,2,1,0:T(8,128)S(1)}, f32[3,8,8,128]{3,2,1,0:T(8,128)}, u32[]{:S(2)}) copy-start(f32[3,8,8,128]{3,2,1,0:T(8,128)} %param.8) | copy-start | bytes 294916
  0.7 37.0 %copy-start.1 = (f32[3,8,8,128]{3,2,1,0:T(8,128)S(1)}, f32[3,8,8,128]{3,2,1,0:T(8,128)}, u32[]{:S(2)}) copy-start(f32[3,8,8,128]{3,2,1,0:T(8,128)} %param.6) | copy-start | bytes 294916
  3.2 6.6 %collective-permute-start = (f32[8,2,8,128]{3,2,1,0:T(8,128)S(1)}, f32[8,2,8,128]{3,2,1,0:T(8,128)S(1)}, u32[]{:S(2)}, u32[]{:S(2)}) collective-permute-start(f32[8,2,8,128]{3,2,1,0:T(8,128)S(1)} %get-tuple-element.66), channel_id=1, source_target_pairs={{0,128},{128,256},{256,384},{384,512},{512,640},{640,768},{768,896... | collective-permute-start | bytes 196616 | tf_op jit(solution)/shard_map/ppermute | solution.py:24
  7.8 7.4 %collective-permute-start.1 = (f32[8,2,8,128]{3,2,1,0:T(8,128)S(1)}, f32[8,2,8,128]{3,2,1,0:T(8,128)S(1)}, u32[]{:S(2)}, u32[]{:S(2)}) collective-permute-start(f32[8,2,8,128]{3,2,1,0:T(8,128)S(1)} %get-tuple-element.67), channel_id=1, source_target_pairs={{128,0},{256,128},{384,256},{512,384},{640,512},{768,640},{896,768... | collective-permute-start | bytes 196616 | tf_op jit(solution)/shard_map/ppermute | solution.py:26
  16.3 20.1 %collective-permute-start.2 = (f32[8,12,2,128]{3,2,1,0:T(2,128)S(1)}, f32[8,12,2,128]{3,2,1,0:T(2,128)S(1)}, u32[]{:S(2)}, u32[]{:S(2)}) collective-permute-start(f32[8,12,2,128]{3,2,1,0:T(2,128)S(1)} %get-tuple-element.64), channel_id=1, source_target_pairs={{0,4},{4,8},{8,12},{12,16},{16,20},{20,24},{24,28},{28,32},{32,36}... | collective-permute-start | bytes 294920 | tf_op jit(solution)/shard_map/ppermute | solution.py:24
  21.5 16.0 %collective-permute-start.3 = (f32[8,12,2,128]{3,2,1,0:T(2,128)S(1)}, f32[8,12,2,128]{3,2,1,0:T(2,128)S(1)}, u32[]{:S(2)}, u32[]{:S(2)}) collective-permute-start(f32[8,12,2,128]{3,2,1,0:T(2,128)S(1)} %get-tuple-element.65), channel_id=1, source_target_pairs={{4,0},{8,4},{12,8},{16,12},{20,16},{24,20},{28,24},{32,28},{36,32}... | collective-permute-start | bytes 294920 | tf_op jit(solution)/shard_map/ppermute | solution.py:26
  39.6 17.0 %collective-permute-start.5 = (f32[8,12,12,2]{2,0,3,1:T(8,128)S(1)}, f32[8,12,12,2]{2,0,3,1:T(8,128)S(1)}, u32[]{:S(2)}, u32[]{:S(2)}) collective-permute-start(f32[8,12,12,2]{2,0,3,1:T(8,128)S(1)} %copy.52), channel_id=1, source_target_pairs={{1,0},{2,1},{3,2},{0,3},{5,4},{6,5},{7,6},{4,7},{9,8},{10,9},{11,1... | collective-permute-start | bytes 27656 | tf_op jit(solution)/shard_map/ppermute | solution.py:26
  45.0 10.9 %collective-permute-start.4 = (f32[8,12,12,2]{2,0,3,1:T(8,128)S(1)}, f32[8,12,12,2]{2,0,3,1:T(8,128)S(1)}, u32[]{:S(2)}, u32[]{:S(2)}) collective-permute-start(f32[8,12,12,2]{2,0,3,1:T(8,128)S(1)} %copy.51), channel_id=1, source_target_pairs={{0,1},{1,2},{2,3},{3,0},{4,5},{5,6},{6,7},{7,4},{8,9},{9,10},{10,1... | collective-permute-start | bytes 27656 | tf_op jit(solution)/shard_map/ppermute | solution.py:24
  66.8 1.9 %copy-start.2 = (f32[12,12,132]{2,1,0:T(8,128)}, f32[12,12,132]{2,1,0:T(8,128)S(1)}, u32[]{:S(2)}) copy-start(f32[12,12,132]{2,1,0:T(8,128)S(1)} %add_multiply_fusion.6) | copy-start | bytes 228100
  69.5 1.2 %copy-start.3 = (f32[12,12,132]{2,1,0:T(8,128)S(1)}, f32[12,12,132]{2,1,0:T(8,128)}, u32[]{:S(2)}) copy-start(f32[12,12,132]{2,1,0:T(8,128)} %copy-done.2) | copy-start | bytes 228100
  69.5 1.2 %slice-start = ((f32[12,12,132]{2,1,0:T(8,128)}), f32[12,12,1]{2,1,0:T(8,128)S(1)}, s32[]{:S(2)}) async-start(f32[12,12,132]{2,1,0:T(8,128)} %copy-done.2), calls=%async_computation | async-start | bytes 196608 | tf_op jit(solution)/shard_map/jit(_roll_static)/slice | solution.py:34
  70.9 0.7 copy-start.5
where the time goes:
time: 72 us; the launch traced here: 71.5 us
  starting transfers between devices  33 us (46%)
  other arithmetic  15.6 us (22%)
  waiting for transfers between devices  15.2 us (21%)
  local copies, waits for them, and re-layouts  6.14 us (9%)
  between operations  1.63 us (2%)
    ppermute x3, starting transfers between devices, with_halo(): lax.ppermute(head, axis, [((i + 1) % count, i) for i in range(ends)])  21.1 us
    ppermute x3, starting transfers between devices, with_halo(): lax.ppermute(tail, axis, [(i, (i + 1) % count) for i in range(ends)])  11.9 us
    ppermute x3, waiting for transfers between devices, with_halo(): lax.ppermute(tail, axis, [(i, (i + 1) % count) for i in range(ends)])  8.78 us
    mul x14, other arithmetic, interface_flux(): (fastest * lower_flux - slowest * upper_flux + slowest * fastest * jump)...  6.56 us
    ppermute x3, waiting for transfers between devices, with_halo(): lax.ppermute(head, axis, [((i + 1) % count, i) for i in range(ends)])  6.37 us
    slice x2, other arithmetic, with_halo(): lax.slice_in_dim(cells, cells.shape[dim] - width, cells.shape[dim], axis=...  1.91 us
  transfers between devices with their start and end apart: 6, of which 3 were waited for; matrix products, arithmetic and copies ran while one was open for 3% of the time, Pallas kernels for 0%

commit v1 on v0

v1 whole, which is shorter than its diff:
```python
import jax
import jax.numpy as jnp
from jax import lax
from jax.experimental import pallas as pl
from jax.experimental.pallas import tpu as pltpu
from jax.sharding import PartitionSpec as P

COOL_STEPS = 8
GAMMA = 5.0 / 3.0
COURANT = 0.08
COOL_RATE = 0.03
GRAVITY = 1.0

NZ, NY, NX = 8, 8, 128
ROWS = 10
UP_ROWS, DOWN_ROWS = 88, 96
Z_MAIN = range(NZ)

f32 = jnp.float32


def gather_block(density, velocity, pressure, field, own, top, bottom, sems):
    one = pl.ds(0, 1)
    copies = []
    for out, z in ((top, NZ - 1), (bottom, 0)):
        copies += [
            (density.at[pl.ds(z, 1)], out.at[one]),
            (velocity.at[:, z], out.at[pl.ds(1, 3)]),
            (pressure.at[pl.ds(z, 1)], out.at[pl.ds(4, 1)]),
            (field.at[:, z], out.at[pl.ds(5, 3)]),
        ]
    copies += [
        (field.at[0, pl.ds(1, 1)], bottom.at[pl.ds(8, 1)]),
        (density, own.at[0]),
        (velocity, own.at[pl.ds(1, 3)]),
        (pressure, own.at[4]),
        (field, own.at[pl.ds(5, 3)]),
    ]
    copies = [pltpu.make_async_copy(a, b, sems.at[i]) for i, (a, b) in enumerate(copies)]
    for copy in copies:
        copy.start()
    for copy in copies:
        copy.wait()


def pack_rows(own, below, above, up, down):
    lowest = lax.axis_index("gz") == 0
    highest = lax.axis_index("gz") == lax.axis_size("gz") - 1

    def put(out, at, row):
        out[pl.ds(at, 1), :] = row

    for out, y in ((up, NY - 1), (down, 0)):
        for member in range(8):
            base = member * ROWS
            for z in Z_MAIN:
                put(out, base + 1 + z, own[member, z, pl.ds(y, 1), :])
            put(out, base, below[member, pl.ds(y, 1), :])
            put(out, base + 9, above[member, pl.ds(y, 1), :])
        put(out, 80, above[8, pl.ds(y, 1), :])
    for z in Z_MAIN:
        put(down, 82 + z, own[6, z, pl.ds(1, 1), :])
    put(down, 81, below[6, pl.ds(1, 1), :])
    put(down, 90, above[6, pl.ds(1, 1), :])

    @pl.when(lowest)
    def _():
        for out, y in ((up, NY - 1), (down, 0)):
            for member in range(8):
                put(out, member * ROWS, own[member, 0, pl.ds(y, 1), :])
        put(down, 81, own[6, 0, pl.ds(1, 1), :])

    @pl.when(highest)
    def _():
        for out, y in ((up, NY - 1), (down, 0)):
            for member in range(8):
                put(out, member * ROWS + 9, own[member, NZ - 1, pl.ds(y, 1), :])
            put(out, 80, own[5, NZ - 1, pl.ds(y, 1), :])
        put(down, 90, own[6, NZ - 1, pl.ds(1, 1), :])


def lanes():
    return lax.broadcasted_iota(jnp.int32, (8, NX), 1)


def sublanes():
    return lax.broadcasted_iota(jnp.int32, (8, NX), 0)


def roll(values, by, axis):
    size = values.shape[axis]
    by = by % size
    return values if by == 0 else pltpu.roll(values, by, axis)


def cool(density, pressure):
    for _ in range(COOL_STEPS):
        pressure = pressure / (1.0 + COOL_RATE * jnp.sqrt(density * pressure))
    return pressure


def pack_columns(corona, own, below, above, left_rows, right_rows, ext, cols):
    row_at, row_count = lax.axis_index("gy"), lax.axis_size("gy")
    slab_at, slab_count = lax.axis_index("gz"), lax.axis_size("gz")
    for member in range(8):
        for z in Z_MAIN:
            ext[member, z + 1, 0:8, :] = own[member, z]
        ext[member, 0, 0:8, :] = below[member]
        ext[member, 9, 0:8, :] = above[member]
    ext[5, 10, 0:8, :] = above[8]

    @pl.when(slab_at == 0)
    def _():
        for member in range(8):
            ext[member, 0, 0:8, :] = own[member, 0]

    @pl.when(slab_at == slab_count - 1)
    def _():
        for member in range(8):
            ext[member, 9, 0:8, :] = own[member, NZ - 1]
        ext[5, 10, 0:8, :] = own[5, NZ - 1]

    where = [(member, z, member * ROWS + z) for member in range(8) for z in range(ROWS)] + [(5, 10, 80)]
    for member, z, at in where:
        ext[member, z, 15:16, :] = left_rows[pl.ds(at, 1), :]
        ext[member, z, 8:9, :] = right_rows[pl.ds(at, 1), :]
    for z in range(ROWS):
        ext[6, z, 9:10, :] = right_rows[pl.ds(81 + z, 1), :]

    @pl.when(row_at == 0)
    def _():
        for member, z, _at in where:
            ext[member, z, 15:16, :] = ext[member, z, 0:1, :]

    @pl.when(row_at == row_count - 1)
    def _():
        for member, z, _at in where:
            ext[member, z, 8:9, :] = ext[member, z, 7:8, :]
        for z in range(ROWS):
            ext[6, z, 9:10, :] = ext[6, z, 7:8, :]

    tiles = [(z, t) for z in range(ROWS) for t in range(2)]
    rho = [ext[0, z, 8 * t : 8 * t + 8, :] for z, t in tiles]
    raw = [ext[4, z, 8 * t : 8 * t + 8, :] for z, t in tiles]
    now = list(raw)
    for _ in range(COOL_STEPS):
        now = [p / (1.0 + COOL_RATE * jnp.sqrt(r * p)) for r, p in zip(rho, now)]
    last = slab_count * NZ - 1
    for (z, t), p, q in zip(tiles, raw, now):
        mark = corona[jnp.clip(slab_at * NZ + z - 1, 0, last)]
        ext[4, z, 8 * t : 8 * t + 8, :] = jnp.where(jnp.full((8, NX), mark, jnp.int32) == 1, q, p)

    lane = lanes()
    for t in range(2):
        rows = slice(8 * t, 8 * t + 8)
        low = jnp.zeros((8, NX), f32)
        high = jnp.zeros((8, NX), f32)
        second = jnp.zeros((8, NX), f32)
        for z in range(11):
            for member in range(8) if z < 10 else (5,):
                at = 8 * z + member
                tile = ext[member, z, rows, :]
                low = jnp.where(lane == at, roll(tile, at, 1), low)
                high = jnp.where(lane == at, roll(tile, at + 1, 1), high)
                if member == 7:
                    second = jnp.where(lane == 8 * z + 2, roll(tile, 8 * z + 1, 1), second)
        cols[0, rows, :] = low
        cols[1, rows, :] = high
        cols[2, rows, :] = second


class Cell:
    def __init__(self, rho, vel, p, cen):
        self.rho, self.vel, self.p, self.cen = rho, vel, p, cen
        self.mom = [rho * v for v in vel]
        kinetic = self.mom[0] * vel[0] + self.mom[1] * vel[1] + self.mom[2] * vel[2]
        self.thermal = p * (1.0 / (GAMMA - 1.0)) + 0.5 * kinetic
        self.inv = 1.0 / rho
        self.sound = GAMMA * p * self.inv


def state(cell, normal, axis):
    b, c = [k for k in range(3) if k != axis]
    vel, cen = cell.vel, cell.cen
    across = cen[b] * cen[b] + cen[c] * cen[c]
    square = normal * normal
    half = 0.5 * (across + square)
    total = cell.p + half
    energy = cell.thermal + half
    n, t, s = square * cell.inv, across * cell.inv, cell.sound
    gap = s - n - t
    fast = jnp.sqrt(0.5 * (s + n + t + jnp.sqrt(gap * gap + 4.0 * s * t)))
    align = vel[axis] * normal + vel[b] * cen[b] + vel[c] * cen[c]
    va = vel[axis]
    flux = [cell.mom[axis]]
    for k in range(3):
        if k == axis:
            flux.append(cell.mom[k] * va - square + total)
        else:
            flux.append(cell.mom[k] * va - cen[k] * normal)
    flux.append((energy + total) * va - normal * align)
    for k in (b, c):
        flux.append(va * cen[k] - vel[k] * normal)
    held = [cell.rho] + cell.mom + [energy, cen[b], cen[c]]
    return va, fast, held, flux


def hll(lower, upper, normal, axis, members):
    lv, lf, lu, lflux = state(lower, normal, axis)
    uv, uf, uu, uflux = state(upper, normal, axis)
    slow = jnp.minimum(jnp.minimum(lv - lf, uv - uf), 0.0)
    fast = jnp.maximum(jnp.maximum(lv + lf, uv + uf), 0.0)
    inverse = 1.0 / (fast - slow)
    a, b = fast * inverse, slow * inverse
    c = slow * a
    return {m: a * lflux[m] - b * uflux[m] + c * (uu[m] - lu[m]) for m in members}


def member_of(axis, component):
    return 5 + [k for k in range(3) if k != axis].index(component)


def advance(gathered, own_cols, ext, conserved, faces_new):
    lane, sub = lanes(), sublanes()
    size = lax.axis_size("gx")
    at = lax.axis_index("gx")
    left, right = lax.rem(at + size - 1, size), lax.rem(at + 1, size)
    first_lane, last_lane = lane == 0, lane == NX - 1
    first_row, last_row = sub == 0, sub == 7
    slot = lane % 8

    def down_y(q):
        r0, r1 = roll(q[0], 1, 0), roll(q[1], 1, 0)
        return [jnp.where(first_row, r1, r0), jnp.where(first_row, r0, r1)]

    def up_y(q):
        r0, r1 = roll(q[0], -1, 0), roll(q[1], -1, 0)
        return [jnp.where(last_row, r1, r0), jnp.where(last_row, r0, r1)]

    def down_x(q, side, source):
        return jnp.where(first_lane, roll(side, -source, 1), roll(q, 1, 1))

    def up_x(q, side, source):
        return jnp.where(last_lane, roll(side, NX - 1 - source, 1), roll(q, -1, 1))

    low_r = [gathered[right, 0, 8 * t : 8 * t + 8, :] for t in range(2)]
    two_r = [gathered[right, 2, 8 * t : 8 * t + 8, :] for t in range(2)]
    high_l = [gathered[left, 1, 8 * t : 8 * t + 8, :] for t in range(2)]
    own_low = [own_cols[0, 8 * t : 8 * t + 8, :] for t in range(2)]
    own_high = [own_cols[1, 8 * t : 8 * t + 8, :] for t in range(2)]

    def column(member):
        out = []
        for t in range(2):
            v = roll(own_high[t], -member, 1)
            v = jnp.where(slot == 1, roll(low_r[t], 1 - member, 1), v)
            v = jnp.where(slot == 3, roll(high_l[t], 3 - member, 1), v)
            v = jnp.where(slot == 4, roll(own_low[t], 4 - member, 1), v)
            if member == 7:
                v = jnp.where(slot == 2, two_r[t], v)
            out.append(v)
        return out

    col = [column(member) for member in range(8)]
    col_next_y = up_y(col[6])
    col_cen = [
        [0.5 * (v + roll(v, -8, 1)) for v in col[5]],
        [0.5 * (v + n) for v, n in zip(col[6], col_next_y)],
        [0.5 * (v + roll(v, -1, 1)) for v in col[7]],
    ]

    def cells(prim, cen):
        return [Cell(prim[0][t], [prim[k][t] for k in (1, 2, 3)], prim[4][t], [cen[k][t] for k in range(3)]) for t in range(2)]

    col_cell = cells(col, col_cen)
    shifted = lambda by: cells(
        [[roll(v, by, 1) for v in col[k]] for k in range(5)],
        [[roll(v, by, 1) for v in col_cen[k]] for k in range(3)],
    )
    full = tuple(range(7))
    col_x_lower, col_z_lower = shifted(1), shifted(8)
    col_y_lower = cells([down_y(col[k]) for k in range(5)], [down_y(col_cen[k]) for k in range(3)])
    XB = {(a, k): member_of(a, k) for a in range(3) for k in range(3) if a != k}
    col_fx = [hll(col_x_lower[0], col_cell[0], col[7][0], 2, full), hll(col_x_lower[1], col_cell[1], col[7][1], 2, (XB[2, 1],))]
    col_fy = [hll(col_y_lower[t], col_cell[t], col[6][t], 1, (XB[1, 2],))[XB[1, 2]] for t in range(2)]
    col_fz = hll(col_z_lower[0], col_cell[0], col[5][0], 0, (XB[0, 2],))[XB[0, 2]]
    fx_by = [f[XB[2, 1]] for f in col_fx]
    fx_bz = col_fx[0][XB[2, 0]]
    down = down_y(fx_by)
    col_ez = [0.25 * (col_fy[t] + roll(col_fy[t], 1, 1) - fx_by[t] - down[t]) for t in range(2)]
    col_ey = 0.25 * (fx_bz + roll(fx_bz, 8, 1) - col_fz - roll(col_fz, 1, 1))

    def slab_cells(z):
        base = 8 * (z + 1)
        get = lambda member, s: [ext[member, s, 0:8, :], ext[member, s, 8:16, :]]
        prim = [get(member, z + 1) for member in range(8)]
        next_z = get(5, z + 2)
        next_y = up_y(prim[6])
        next_x = [up_x(prim[7][t], low_r[t], base + 7) for t in range(2)]
        cen = [
            [0.5 * (prim[5][t] + next_z[t]) for t in range(2)],
            [0.5 * (prim[6][t] + next_y[t]) for t in range(2)],
            [0.5 * (prim[7][t] + next_x[t]) for t in range(2)],
        ]
        return prim, cen, cells(prim, cen)

    def slab_fluxes(z, prim, cen, here, below):
        base = 8 * (z + 1)
        inside = 0 <= z < NZ
        fz = fy = fx = None
        if z >= 0:
            fz = [
                hll(below[0], here[0], prim[5][0], 0, full),
                hll(below[1], here[1], prim[5][1], 0, (XB[0, 1],)),
            ]
        y_lower = cells([down_y(prim[k]) for k in range(5)], [down_y(cen[k]) for k in range(3)])
        x_lower = []
        for t in range(2):
            p = [down_x(prim[k][t], high_l[t], base + k) for k in range(5)]
            c = [down_x(cen[k][t], col_cen[k][t], base + 3) for k in range(3)]
            x_lower.append(Cell(p[0], p[1:4], p[4], c))
        members = full if inside else (XB[1, 0],)
        fy = [hll(y_lower[t], here[t], prim[6][t], 1, members) for t in range(2)]
        if inside:
            fx = [
                hll(x_lower[0], here[0], prim[7][0], 2, full),
                hll(x_lower[1], here[1], prim[7][1], 2, (XB[2, 1],)),
            ]
        else:
            fx = [hll(x_lower[0], here[0], prim[7][0], 2, (XB[2, 0],)), None]
        return fz, fy, fx

    slabs = lax.axis_size("gz") * NZ
    first_slab = lax.axis_index("gz") * NZ
    previous = None
    for z in range(-1, NZ + 1):
        base = 8 * (z + 1)
        prim, cen, here = slab_cells(z)
        below = previous["here"] if previous else None
        fz, fy, fx = slab_fluxes(z, prim, cen, here, below)
        now = dict(prim=prim, cen=cen, here=here, fz=fz, fy=fy, fx=fx, base=base)
        if z >= 0:
            by = [fz[t][XB[0, 1]] for t in range(2)]
            by_down = down_y(by)
            now["ex"] = [0.25 * (by[t] + by_down[t] - fy[t][XB[1, 0]] - previous["fy"][t][XB[1, 0]]) for t in range(2)]
            bx = fz[0][XB[0, 2]]
            now["ey"] = 0.25 * (fx[0][XB[2, 0]] + previous["fx"][0][XB[2, 0]] - bx - down_x(bx, col_fz, base + 3))
        if 0 <= z < NZ:
            bx = [fy[t][XB[1, 2]] for t in range(2)]
            by = [fx[t][XB[2, 1]] for t in range(2)]
            by_down = down_y(by)
            now["ez"] = [0.25 * (bx[t] + down_x(bx[t], col_fy[t], base + 3) - by[t] - by_down[t]) for t in range(2)]
        if z >= 1:
            k = z - 1
            was = previous
            cell = was["here"][0]
            pull = -GRAVITY * (2 * (first_slab + k) + 1 - slabs).astype(f32) / slabs
            squared = sum(c[0] * c[0] for c in was["cen"])
            held = [cell.rho] + cell.mom + [cell.thermal + 0.5 * squared]
            for m in range(5):
                y_next = up_y([was["fy"][t][m] for t in range(2)])[0]
                x_next = up_x(was["fx"][0][m], col_fx[0][m], was["base"] + 1)
                change = (fz[0][m] - was["fz"][0][m]) + (y_next - was["fy"][0][m]) + (x_next - was["fx"][0][m])
                value = held[m] - COURANT * change
                if m == 1:
                    value = value + (COURANT * pull) * cell.rho
                if m == 4:
                    value = value + (COURANT * pull) * cell.mom[0]
                conserved[m, k] = value
            ex, ey, ez = was["ex"], was["ey"], was["ez"]
            ex_up_y, ez_up_y = up_y(ex)[0], up_y(ez)[0]
            ey_up_x = up_x(ey, col_ey, was["base"] + 1)
            ez_up_x = up_x(ez[0], col_ez[0], was["base"] + 1)
            curls = (
                ey_up_x - ey - (ex_up_y - ex[0]),
                now["ex"][0] - ex[0] - (ez_up_x - ez[0]),
                ez_up_y - ez[0] - (now["ey"] - ey),
            )
            for c in range(3):
                faces_new[c, k] = was["prim"][5 + c][0] - COURANT * curls[c]
        previous = now


VMEM = pl.BlockSpec(memory_space=pltpu.VMEM)
SMEM = pl.BlockSpec(memory_space=pltpu.SMEM)


def shape(*dims):
    return jax.ShapeDtypeStruct(dims, f32)


def held(*dims):
    return pltpu.VMEM(dims, f32)


def near(*arrays):
    return [pltpu.with_memory_space_constraint(a, pltpu.VMEM) for a in arrays]


def neighbours(axis):
    count = lax.axis_size(axis)
    return [(i, i + 1) for i in range(count - 1)], [(i + 1, i) for i in range(count - 1)]


def on_device(density, velocity, pressure, field, corona):
    own, top, bottom = pl.pallas_call(
        gather_block,
        out_shape=(held(8, NZ, NY, NX), held(8, NY, NX), held(9, NY, NX)),
        in_specs=[pl.BlockSpec(memory_space=pl.ANY)] * 4,
        out_specs=(VMEM,) * 3,
        scratch_shapes=[pltpu.SemaphoreType.DMA((13,))],
        name="gather_block",
    )(density, velocity, pressure, field)
    up, down = neighbours("gz")
    below = lax.ppermute(top, "gz", up)
    above = lax.ppermute(bottom, "gz", down)
    rows_up, rows_down = pl.pallas_call(
        pack_rows,
        out_shape=(held(UP_ROWS, NX), held(DOWN_ROWS, NX)),
        in_specs=[VMEM] * 3,
        out_specs=(VMEM, VMEM),
        name="pack_rows",
    )(*near(own, below, above))
    up, down = neighbours("gy")
    left_rows = lax.ppermute(rows_up, "gy", up)
    right_rows = lax.ppermute(rows_down, "gy", down)
    ext, cols = pl.pallas_call(
        pack_columns,
        out_shape=(held(8, 11, 16, NX), held(3, 16, NX)),
        in_specs=[SMEM] + [VMEM] * 5,
        out_specs=(VMEM, VMEM),
        name="pack_columns",
    )(corona, *near(own, below, above, left_rows, right_rows))
    gathered = lax.all_gather(cols, "gx", axis=0)
    return pl.pallas_call(
        advance,
        out_shape=(shape(5, NZ, NY, NX), shape(3, NZ, NY, NX)),
        in_specs=[VMEM] * 3,
        out_specs=(VMEM, VMEM),
        name="advance",
    )(*near(gathered, cols, ext))


def solution(mesh):
    block = P("gz", "gy", "gx")
    blocks = P(None, "gz", "gy", "gx")
    return jax.shard_map(
        on_device,
        mesh=mesh,
        in_specs=(block, blocks, block, blocks, P()),
        out_specs=(blocks, blocks),
        check_vma=False,
    )
```

time: 72 us -> 51.1 us (0.71)
  the two profiles are of different devices: /device:TPU:22 before, /device:TPU:105 now
where the time goes in v1:
time: 51.1 us; the launch traced here: 50.9 us
  starting transfers between devices  24.9 us (49%)
  blocking collectives  12.6 us (25%)
  waiting for transfers between devices  7.72 us (15%)
  Pallas kernels  4.94 us (10%)
  between operations  0.68 us (1%)
    ppermute x1, starting transfers between devices, on_device(): right_rows = lax.ppermute(rows_down, 'gy', down)  17.7 us
    all_gather x1, blocking collectives, on_device(): gathered = lax.all_gather(cols, 'gx', axis=0)  12.6 us
    ppermute x1, waiting for transfers between devices, on_device(): left_rows = lax.ppermute(rows_up, 'gy', up)  4.97 us
    ppermute x1, starting transfers between devices, on_device(): below = lax.ppermute(top, 'gz', up)  3.12 us
    ppermute x1, waiting for transfers between devices, on_device(): below = lax.ppermute(top, 'gz', up)  2.74 us
    pallas_call x1, Pallas kernels, on_device(): pl.pallas_call(advance, out_shape=(shape(5, NZ, NY, NX), shape(3, NZ, NY,...  2.39 us
    ppermute x1, starting transfers between devices, on_device(): above = lax.ppermute(bottom, 'gz', down)  2.16 us
    ppermute x1, starting transfers between devices, on_device(): left_rows = lax.ppermute(rows_up, 'gy', up)  1.92 us
  transfers between devices with their start and end apart: 4, of which 2 were waited for; matrix products, arithmetic and copies ran while one was open for 0% of the time, Pallas kernels for 0%

profile of v1, /device:TPU:105, one launch (start us, length us, event | category | flops | bytes accessed | tf_op | source)
XLA Modules:
  0.0 50.9 jit_solution(16068903684621928642)
XLA Ops:
  0.6 1.2 %gather_block.1 = (f32[8,8,8,128]{3,2,1,0:T(8,128)S(1)}, f32[8,8,128]{2,1,0:T(8,128)S(1)}, f32[9,8,128]{2,1,0:T(8,128)S(1)}) custom-call(f32[8,8,128]{2,1,0:T(8,128)} %density.1, f32[3,8,8,128]{3,2,1,0:T(8,128)} %velocity.1, f32[8,8,128]{2,1,0:T(8,128)} %pressure.1, f32[3,8,8,128]{3,2,1,0:T(8,128)} %field.1), custom_call_target="tpu_custom_call" | custom-call | tf_op jit(solution)/shard_map/gather_block/pallas_call | solution.py:406
  1.9 2.2 %collective-permute-start.1 = (f32[9,8,128]{2,1,0:T(8,128)S(1)}, f32[9,8,128]{2,1,0:T(8,128)S(1)}, u32[]{:S(2)}, u32[]{:S(2)}) collective-permute-start(f32[9,8,128]{2,1,0:T(8,128)S(1)} %get-tuple-element.11), channel_id=1, source_target_pairs={{128,0},{256,128},{384,256},{512,384},{640,512},{768,640},{896,768... | collective-permute-start | bytes 110600 | tf_op jit(solution)/shard_map/ppermute | solution.py:416
  4.0 3.1 %collective-permute-start = (f32[8,8,128]{2,1,0:T(8,128)S(1)}, f32[8,8,128]{2,1,0:T(8,128)S(1)}, u32[]{:S(2)}, u32[]{:S(2)}) collective-permute-start(f32[8,8,128]{2,1,0:T(8,128)S(1)} %get-tuple-element.10), channel_id=1, source_target_pairs={{0,128},{128,256},{256,384},{384,512},{512,640},{640,768},{768,896... | collective-permute-start | bytes 98312 | tf_op jit(solution)/shard_map/ppermute | solution.py:415
  7.2 2.7 %collective-permute-done.below = f32[8,8,128]{2,1,0:T(8,128)S(1)} collective-permute-done((f32[8,8,128]{2,1,0:T(8,128)S(1)}, f32[8,8,128]{2,1,0:T(8,128)S(1)}, u32[]{:S(2)}, u32[]{:S(2)}) %collective-permute-start) | collective-permute-done | bytes 32800 | tf_op jit(solution)/shard_map/ppermute | solution.py:415
  9.9 0.0 collective-permute-done.1.above
  9.9 0.1 pack_rows.1
  10.0 17.7 %collective-permute-start.3 = (f32[96,128]{1,0:T(8,128)S(1)}, f32[96,128]{1,0:T(8,128)S(1)}, u32[]{:S(2)}, u32[]{:S(2)}) collective-permute-start(f32[96,128]{1,0:T(8,128)S(1)} %get-tuple-element.13), channel_id=1, source_target_pairs={{4,0},{8,4},{12,8},{16,12},{20,16},{24,20},{28,24},{32,28},{36,32}... | collective-permute-start | bytes 147464 | tf_op jit(solution)/shard_map/ppermute | solution.py:426
  27.7 1.9 %collective-permute-start.2 = (f32[88,128]{1,0:T(8,128)S(1)}, f32[88,128]{1,0:T(8,128)S(1)}, u32[]{:S(2)}, u32[]{:S(2)}) collective-permute-start(f32[88,128]{1,0:T(8,128)S(1)} %get-tuple-element.12), channel_id=1, source_target_pairs={{0,4},{4,8},{8,12},{12,16},{16,20},{20,24},{24,28},{28,32},{32,36}... | collective-permute-start | bytes 135176 | tf_op jit(solution)/shard_map/ppermute | solution.py:425
  29.6 5.0 %collective-permute-done.2.left_rows = f32[88,128]{1,0:T(8,128)S(1)} collective-permute-done((f32[88,128]{1,0:T(8,128)S(1)}, f32[88,128]{1,0:T(8,128)S(1)}, u32[]{:S(2)}, u32[]{:S(2)}) %collective-permute-start.2) | collective-permute-done | bytes 45088 | tf_op jit(solution)/shard_map/ppermute | solution.py:425
  34.6 0.0 collective-permute-done.3.right_rows
  34.6 1.3 %pack_columns.1 = (f32[8,11,16,128]{3,2,1,0:T(8,128)S(1)}, f32[3,16,128]{2,1,0:T(8,128)S(1)}) custom-call(s32[64]{0:T(128)} %corona.1, f32[8,8,8,128]{3,2,1,0:T(8,128)S(1)} %get-tuple-element.9.own, f32[8,8,128]{2,1,0:T(8,128)S(1)} %collective-permute-done.below, f32[9,8,128]{2,1,0:T(8,128)S(1)} %collective-permute-done.1.above, ...), custom_call_target="tpu_custom_call" | custom-call | tf_op jit(solution)/shard_map/pack_columns/pallas_call | solution.py:427
  35.9 12.6 %all-gather = f32[12,16,128]{2,1,0:T(8,128)S(1)} all-gather(f32[3,16,128]{2,1,0:T(8,128)S(1)} %get-tuple-element.14.own_cols), channel_id=2, replica_groups=mesh['gz'=8,'gy'=32,'gx'=4] {'gx'}, dimensions={0}, use_global_device_ids=true | all-gather | bytes 122880 | tf_op jit(solution)/shard_map/all_gather | solution.py:434
  48.5 2.4 %advance.1 = (f32[5,8,8,128]{3,2,1,0:T(8,128)}, f32[3,8,8,128]{3,2,1,0:T(8,128)}) custom-call(f32[4,3,16,128]{3,2,1,0:T(8,128)S(1)} %bitcast.1, f32[3,16,128]{2,1,0:T(8,128)S(1)} %get-tuple-element.14.own_cols, f32[8,11,16,128]{3,2,1,0:T(8,128)S(1)} %get-tuple-element.15.ext), custom_call_target="tpu_custom_call" | custom-call | tf_op jit(solution)/shard_map/advance/pallas_call | solution.py:435
Async XLA Ops:
  1.9 8.0 %collective-permute-start.1 = (f32[9,8,128]{2,1,0:T(8,128)S(1)}, f32[9,8,128]{2,1,0:T(8,128)S(1)}, u32[]{:S(2)}, u32[]{:S(2)}) collective-permute-start(f32[9,8,128]{2,1,0:T(8,128)S(1)} %get-tuple-element.11), channel_id=1, source_target_pairs={{128,0},{256,128},{384,256},{512,384},{640,512},{768,640},{896,768... | collective-permute-start | bytes 110600 | tf_op jit(solution)/shard_map/ppermute | solution.py:416
  4.0 5.9 %collective-permute-start = (f32[8,8,128]{2,1,0:T(8,128)S(1)}, f32[8,8,128]{2,1,0:T(8,128)S(1)}, u32[]{:S(2)}, u32[]{:S(2)}) collective-permute-start(f32[8,8,128]{2,1,0:T(8,128)S(1)} %get-tuple-element.10), channel_id=1, source_target_pairs={{0,128},{128,256},{256,384},{384,512},{512,640},{640,768},{768,896... | collective-permute-start | bytes 98312 | tf_op jit(solution)/shard_map/ppermute | solution.py:415
  10.0 24.6 %collective-permute-start.3 = (f32[96,128]{1,0:T(8,128)S(1)}, f32[96,128]{1,0:T(8,128)S(1)}, u32[]{:S(2)}, u32[]{:S(2)}) collective-permute-start(f32[96,128]{1,0:T(8,128)S(1)} %get-tuple-element.13), channel_id=1, source_target_pairs={{4,0},{8,4},{12,8},{16,12},{20,16},{24,20},{28,24},{32,28},{36,32}... | collective-permute-start | bytes 147464 | tf_op jit(solution)/shard_map/ppermute | solution.py:426
  27.7 6.9 %collective-permute-start.2 = (f32[88,128]{1,0:T(8,128)S(1)}, f32[88,128]{1,0:T(8,128)S(1)}, u32[]{:S(2)}, u32[]{:S(2)}) collective-permute-start(f32[88,128]{1,0:T(8,128)S(1)} %get-tuple-element.12), channel_id=1, source_target_pairs={{0,4},{4,8},{8,12},{12,16},{16,20},{20,24},{24,28},{28,32},{32,36}... | collective-permute-start | bytes 135176 | tf_op jit(solution)/shard_map/ppermute | solution.py:425

commit v2 on v1

--- a/solution.py
+++ b/solution.py
@@ -4,6 +4,7 @@
 from jax.experimental import pallas as pl
 from jax.experimental.pallas import tpu as pltpu
 from jax.sharding import PartitionSpec as P
+
 
 COOL_STEPS = 8
 GAMMA = 5.0 / 3.0
@@ -93,80 +94,87 @@
     return values if by == 0 else pltpu.roll(values, by, axis)
 
 
-def cool(density, pressure):
+def marks_of(corona):
+    first, last = lax.axis_index("gz") * NZ, lax.axis_size("gz") * NZ - 1
+    return [corona[jnp.clip(first + z - 1, 0, last)] for z in range(ROWS)]
+
+
+def cool(corona, ext):
+    rho = [ext[0, z] for z in range(ROWS)]
+    raw = [ext[4, z] for z in range(ROWS)]
+    now = list(raw)
     for _ in range(COOL_STEPS):
-        pressure = pressure / (1.0 + COOL_RATE * jnp.sqrt(density * pressure))
-    return pressure
-
-
-def pack_columns(corona, own, below, above, left_rows, right_rows, ext, cols):
-    row_at, row_count = lax.axis_index("gy"), lax.axis_size("gy")
+        now = [p / (1.0 + COOL_RATE * jnp.sqrt(r * p)) for r, p in zip(rho, now)]
+    for z, (mark, p, q) in enumerate(zip(marks_of(corona), raw, now)):
+        ext[4, z] = jnp.where(jnp.full((8, NX), mark, jnp.int32) == 1, q, p)
+
+
+def columns_of(ext):
+    lane = lanes()
+    low = high = second = jnp.zeros((8, NX), f32)
+    for z in range(11):
+        for member in range(8) if z < 10 else (5,):
+            at = 8 * z + member
+            tile = ext[member, z]
+            low = jnp.where(lane == at, roll(tile, at, 1), low)
+            high = jnp.where(lane == at, roll(tile, at + 1, 1), high)
+            if member == 7:
+                second = jnp.where(lane == 8 * z + 2, roll(tile, 8 * z + 1, 1), second)
+    return low, high, second
+
+
+def pack_main(corona, own, below, above, ext, cols):
     slab_at, slab_count = lax.axis_index("gz"), lax.axis_size("gz")
     for member in range(8):
         for z in Z_MAIN:
-            ext[member, z + 1, 0:8, :] = own[member, z]
-        ext[member, 0, 0:8, :] = below[member]
-        ext[member, 9, 0:8, :] = above[member]
-    ext[5, 10, 0:8, :] = above[8]
+            ext[member, z + 1] = own[member, z]
+        ext[member, 0] = below[member]
+        ext[member, 9] = above[member]
+    ext[5, 10] = above[8]
 
     @pl.when(slab_at == 0)
     def _():
         for member in range(8):
-            ext[member, 0, 0:8, :] = own[member, 0]
+            ext[member, 0] = own[member, 0]
 
     @pl.when(slab_at == slab_count - 1)
     def _():
         for member in range(8):
-            ext[member, 9, 0:8, :] = own[member, NZ - 1]
-        ext[5, 10, 0:8, :] = own[5, NZ - 1]
-
-    where = [(member, z, member * ROWS + z) for member in range(8) for z in range(ROWS)] + [(5, 10, 80)]
-    for member, z, at in where:
-        ext[member, z, 15:16, :] = left_rows[pl.ds(at, 1), :]
-        ext[member, z, 8:9, :] = right_rows[pl.ds(at, 1), :]
+            ext[member, 9] = own[member, NZ - 1]
+        ext[5, 10] = own[5, NZ - 1]
+
+    cool(corona, ext)
+    for i, v in enumerate(columns_of(ext)):
+        cols[i] = v
+
+
+PLACES = [(member, z, member * ROWS + z) for member in range(8) for z in range(ROWS)] + [(5, 10, 80)]
+
+
+def pack_edges(corona, main, main_cols, left_rows, right_rows, ext, cols):
+    row_at, row_count = lax.axis_index("gy"), lax.axis_size("gy")
+    for member, z, at in PLACES:
+        ext[member, z, 7:8, :] = left_rows[pl.ds(at, 1), :]
+        ext[member, z, 0:1, :] = right_rows[pl.ds(at, 1), :]
     for z in range(ROWS):
-        ext[6, z, 9:10, :] = right_rows[pl.ds(81 + z, 1), :]
+        ext[6, z, 1:2, :] = right_rows[pl.ds(81 + z, 1), :]
+    cool(corona, ext)
 
     @pl.when(row_at == 0)
     def _():
-        for member, z, _at in where:
-            ext[member, z, 15:16, :] = ext[member, z, 0:1, :]
+        for member, z, _at in PLACES:
+            ext[member, z, 7:8, :] = main[member, z, 0:1, :]
 
     @pl.when(row_at == row_count - 1)
     def _():
-        for member, z, _at in where:
-            ext[member, z, 8:9, :] = ext[member, z, 7:8, :]
+        for member, z, _at in PLACES:
+            ext[member, z, 0:1, :] = main[member, z, 7:8, :]
         for z in range(ROWS):
-            ext[6, z, 9:10, :] = ext[6, z, 7:8, :]
-
-    tiles = [(z, t) for z in range(ROWS) for t in range(2)]
-    rho = [ext[0, z, 8 * t : 8 * t + 8, :] for z, t in tiles]
-    raw = [ext[4, z, 8 * t : 8 * t + 8, :] for z, t in tiles]
-    now = list(raw)
-    for _ in range(COOL_STEPS):
-        now = [p / (1.0 + COOL_RATE * jnp.sqrt(r * p)) for r, p in zip(rho, now)]
-    last = slab_count * NZ - 1
-    for (z, t), p, q in zip(tiles, raw, now):
-        mark = corona[jnp.clip(slab_at * NZ + z - 1, 0, last)]
-        ext[4, z, 8 * t : 8 * t + 8, :] = jnp.where(jnp.full((8, NX), mark, jnp.int32) == 1, q, p)
-
-    lane = lanes()
-    for t in range(2):
-        rows = slice(8 * t, 8 * t + 8)
-        low = jnp.zeros((8, NX), f32)
-        high = jnp.zeros((8, NX), f32)
-        second = jnp.zeros((8, NX), f32)
-        for z in range(11):
-            for member in range(8) if z < 10 else (5,):
-                at = 8 * z + member
-                tile = ext[member, z, rows, :]
-                low = jnp.where(lane == at, roll(tile, at, 1), low)
-                high = jnp.where(lane == at, roll(tile, at + 1, 1), high)
-                if member == 7:
-                    second = jnp.where(lane == 8 * z + 2, roll(tile, 8 * z + 1, 1), second)
-        cols[0, rows, :] = low
-        cols[1, rows, :] = high
-        cols[2, rows, :] = second
+            ext[6, z, 1:2, :] = main[6, z, 7:8, :]
+
+    for i, v in enumerate(columns_of(ext)):
+        cols[i, 0:8, :] = main_cols[i]
+        cols[i, 8:16, :] = v
 
 
 class Cell:
@@ -220,7 +228,7 @@
     return 5 + [k for k in range(3) if k != axis].index(component)
 
 
-def advance(gathered, own_cols, ext, conserved, faces_new):
+def advance(gathered, own_cols, main, edges, conserved_out, faces_out, conserved, faces_new, sems):
     lane, sub = lanes(), sublanes()
     size = lax.axis_size("gx")
     at = lax.axis_index("gx")
@@ -292,7 +300,7 @@
 
     def slab_cells(z):
         base = 8 * (z + 1)
-        get = lambda member, s: [ext[member, s, 0:8, :], ext[member, s, 8:16, :]]
+        get = lambda member, s: [main[member, s], edges[member, s]]
         prim = [get(member, z + 1) for member in range(8)]
         next_z = get(5, z + 2)
         next_y = up_y(prim[6])
@@ -333,6 +341,7 @@
     slabs = lax.axis_size("gz") * NZ
     first_slab = lax.axis_index("gz") * NZ
     previous = None
+    copies = []
     for z in range(-1, NZ + 1):
         base = 8 * (z + 1)
         prim, cen, here = slab_cells(z)
@@ -378,7 +387,13 @@
             )
             for c in range(3):
                 faces_new[c, k] = was["prim"][5 + c][0] - COURANT * curls[c]
+            for i, (here_at, there) in enumerate(((conserved, conserved_out), (faces_new, faces_out))):
+                copy = pltpu.make_async_copy(here_at.at[:, k], there.at[:, k], sems.at[2 * k + i])
+                copy.start()
+                copies.append(copy)
         previous = now
+    for copy in copies:
+        copy.wait()
 
 
 VMEM = pl.BlockSpec(memory_space=pltpu.VMEM)
@@ -424,21 +439,33 @@
     up, down = neighbours("gy")
     left_rows = lax.ppermute(rows_up, "gy", up)
     right_rows = lax.ppermute(rows_down, "gy", down)
-    ext, cols = pl.pallas_call(
-        pack_columns,
-        out_shape=(held(8, 11, 16, NX), held(3, 16, NX)),
-        in_specs=[SMEM] + [VMEM] * 5,
+    main, main_cols = pl.pallas_call(
+        pack_main,
+        out_shape=(held(8, 11, 8, NX), held(3, 8, NX)),
+        in_specs=[SMEM] + [VMEM] * 3,
         out_specs=(VMEM, VMEM),
-        name="pack_columns",
-    )(corona, *near(own, below, above, left_rows, right_rows))
+        name="pack_main",
+    )(corona, *near(own, below, above))
+    edges, cols = pl.pallas_call(
+        pack_edges,
+        out_shape=(held(8, 11, 8, NX), held(3, 16, NX)),
+        in_specs=[SMEM] + [VMEM] * 4,
+        out_specs=(VMEM, VMEM),
+        name="pack_edges",
+    )(corona, *near(main, main_cols, left_rows, right_rows))
     gathered = lax.all_gather(cols, "gx", axis=0)
     return pl.pallas_call(
         advance,
         out_shape=(shape(5, NZ, NY, NX), shape(3, NZ, NY, NX)),
-        in_specs=[VMEM] * 3,
-        out_specs=(VMEM, VMEM),
+        in_specs=[VMEM] * 4,
+        out_specs=(pl.BlockSpec(memory_space=pl.ANY),) * 2,
+        scratch_shapes=[
+            pltpu.VMEM((5, NZ, NY, NX), f32),
+            pltpu.VMEM((3, NZ, NY, NX), f32),
+            pltpu.SemaphoreType.DMA((2 * NZ,)),
+        ],
         name="advance",
-    )(*near(gathered, cols, ext))
+    )(*near(gathered, cols, main, edges))
 
 
 def solution(mesh):

time: 51.1 us -> 51 us (level)
  the two profiles are of different devices: /device:TPU:105 before, /device:TPU:121 now
where the time goes in v2:
time: 51 us; the launch traced here: 50.8 us
  starting transfers between devices  24.9 us (49%)
  blocking collectives  12.6 us (25%)
  waiting for transfers between devices  6.76 us (13%)
  Pallas kernels  5.8 us (11%)
  between operations  0.69 us (1%)
    ppermute x1, starting transfers between devices, on_device(): right_rows = lax.ppermute(rows_down, 'gy', down)  17.7 us
    all_gather x1, blocking collectives, on_device(): gathered = lax.all_gather(cols, 'gx', axis=0)  12.6 us
    ppermute x1, waiting for transfers between devices, on_device(): left_rows = lax.ppermute(rows_up, 'gy', up)  4.01 us
    ppermute x1, starting transfers between devices, on_device(): below = lax.ppermute(top, 'gz', up)  3.12 us
    ppermute x1, waiting for transfers between devices, on_device(): below = lax.ppermute(top, 'gz', up)  2.74 us
    pallas_call x1, Pallas kernels, on_device(): pl.pallas_call(advance, out_shape=(shape(5, NZ, NY, NX), shape(3, NZ, NY,...  2.41 us
    ppermute x1, starting transfers between devices, on_device(): above = lax.ppermute(bottom, 'gz', down)  2.16 us
    ppermute x1, starting transfers between devices, on_device(): left_rows = lax.ppermute(rows_up, 'gy', up)  1.92 us
  transfers between devices with their start and end apart: 4, of which 2 were waited for; matrix products, arithmetic and copies ran while one was open for 0% of the time, Pallas kernels for 2%

profile of v2, /device:TPU:121, one launch (start us, length us, event | category | flops | bytes accessed | tf_op | source)
XLA Modules:
  0.0 50.8 jit_solution(5107705935450623087)
XLA Ops:
  0.6 1.2 %gather_block.1 = (f32[8,8,8,128]{3,2,1,0:T(8,128)S(1)}, f32[8,8,128]{2,1,0:T(8,128)S(1)}, f32[9,8,128]{2,1,0:T(8,128)S(1)}) custom-call(f32[8,8,128]{2,1,0:T(8,128)} %density.1, f32[3,8,8,128]{3,2,1,0:T(8,128)} %velocity.1, f32[8,8,128]{2,1,0:T(8,128)} %pressure.1, f32[3,8,8,128]{3,2,1,0:T(8,128)} %field.1), custom_call_target="tpu_custom_call" | custom-call | tf_op jit(solution)/shard_map/gather_block/pallas_call | solution.py:421
  1.9 2.2 %collective-permute-start.1 = (f32[9,8,128]{2,1,0:T(8,128)S(1)}, f32[9,8,128]{2,1,0:T(8,128)S(1)}, u32[]{:S(2)}, u32[]{:S(2)}) collective-permute-start(f32[9,8,128]{2,1,0:T(8,128)S(1)} %get-tuple-element.13), channel_id=1, source_target_pairs={{128,0},{256,128},{384,256},{512,384},{640,512},{768,640},{896,768... | collective-permute-start | bytes 110600 | tf_op jit(solution)/shard_map/ppermute | solution.py:431
  4.0 3.1 %collective-permute-start = (f32[8,8,128]{2,1,0:T(8,128)S(1)}, f32[8,8,128]{2,1,0:T(8,128)S(1)}, u32[]{:S(2)}, u32[]{:S(2)}) collective-permute-start(f32[8,8,128]{2,1,0:T(8,128)S(1)} %get-tuple-element.12), channel_id=1, source_target_pairs={{0,128},{128,256},{256,384},{384,512},{512,640},{640,768},{768,896... | collective-permute-start | bytes 98312 | tf_op jit(solution)/shard_map/ppermute | solution.py:430
  7.2 2.7 %collective-permute-done.below = f32[8,8,128]{2,1,0:T(8,128)S(1)} collective-permute-done((f32[8,8,128]{2,1,0:T(8,128)S(1)}, f32[8,8,128]{2,1,0:T(8,128)S(1)}, u32[]{:S(2)}, u32[]{:S(2)}) %collective-permute-start) | collective-permute-done | bytes 32800 | tf_op jit(solution)/shard_map/ppermute | solution.py:430
  9.9 0.0 collective-permute-done.1.above
  9.9 0.1 pack_rows.1
  10.0 17.7 %collective-permute-start.3 = (f32[96,128]{1,0:T(8,128)S(1)}, f32[96,128]{1,0:T(8,128)S(1)}, u32[]{:S(2)}, u32[]{:S(2)}) collective-permute-start(f32[96,128]{1,0:T(8,128)S(1)} %get-tuple-element.17), channel_id=1, source_target_pairs={{4,0},{8,4},{12,8},{16,12},{20,16},{24,20},{28,24},{32,28},{36,32}... | collective-permute-start | bytes 147464 | tf_op jit(solution)/shard_map/ppermute | solution.py:441
  27.7 1.9 %collective-permute-start.2 = (f32[88,128]{1,0:T(8,128)S(1)}, f32[88,128]{1,0:T(8,128)S(1)}, u32[]{:S(2)}, u32[]{:S(2)}) collective-permute-start(f32[88,128]{1,0:T(8,128)S(1)} %get-tuple-element.16), channel_id=1, source_target_pairs={{0,4},{4,8},{8,12},{12,16},{16,20},{20,24},{24,28},{28,32},{32,36}... | collective-permute-start | bytes 135176 | tf_op jit(solution)/shard_map/ppermute | solution.py:440
  29.6 1.0 %pack_main.1 = (f32[8,11,8,128]{3,2,1,0:T(8,128)S(1)}, f32[3,8,128]{2,1,0:T(8,128)S(1)}) custom-call(s32[64]{0:T(128)} %corona.3, f32[8,8,8,128]{3,2,1,0:T(8,128)S(1)} %get-tuple-element.11.own, f32[8,8,128]{2,1,0:T(8,128)S(1)} %collective-permute-done.below, f32[9,8,128]{2,1,0:T(8,128)S(1)} %collective-permute-done.1.above), custom_call_target="tpu_custom_call" | custom-call | tf_op jit(solution)/shard_map/pack_main/pallas_call | solution.py:442
  30.6 4.0 %collective-permute-done.2.left_rows = f32[88,128]{1,0:T(8,128)S(1)} collective-permute-done((f32[88,128]{1,0:T(8,128)S(1)}, f32[88,128]{1,0:T(8,128)S(1)}, u32[]{:S(2)}, u32[]{:S(2)}) %collective-permute-start.2) | collective-permute-done | bytes 45088 | tf_op jit(solution)/shard_map/ppermute | solution.py:440
  34.6 0.0 collective-permute-done.3.right_rows
  34.6 1.1 %pack_edges.1 = (f32[8,11,8,128]{3,2,1,0:T(8,128)S(1)}, f32[3,16,128]{2,1,0:T(8,128)S(1)}) custom-call(s32[64]{0:T(128)} %corona.3, f32[8,11,8,128]{3,2,1,0:T(8,128)S(1)} %get-tuple-element.14.main, f32[3,8,128]{2,1,0:T(8,128)S(1)} %get-tuple-element.15.main_cols, f32[88,128]{1,0:T(8,128)S(1)} %collective-permute-done.2.left_rows, ...), custom_call_target="tpu_custom_call" | custom-call | tf_op jit(solution)/shard_map/pack_edges/pallas_call | solution.py:449
  35.7 12.6 %all-gather = f32[12,16,128]{2,1,0:T(8,128)S(1)} all-gather(f32[3,16,128]{2,1,0:T(8,128)S(1)} %get-tuple-element.18.own_cols), channel_id=2, replica_groups=mesh['gz'=8,'gy'=32,'gx'=4] {'gx'}, dimensions={0}, use_global_device_ids=true | all-gather | bytes 122880 | tf_op jit(solution)/shard_map/all_gather | solution.py:456
  48.3 2.4 %advance.1 = (f32[5,8,8,128]{3,2,1,0:T(8,128)}, f32[3,8,8,128]{3,2,1,0:T(8,128)}) custom-call(f32[4,3,16,128]{3,2,1,0:T(8,128)S(1)} %bitcast.1, f32[3,16,128]{2,1,0:T(8,128)S(1)} %get-tuple-element.18.own_cols, f32[8,11,8,128]{3,2,1,0:T(8,128)S(1)} %get-tuple-element.14.main, f32[8,11,8,128]{3,2,1,0:T(8,128)S(1)} %get-tuple-element.19.edges), custom_call_target="tpu_custom_call" | custom-call | tf_op jit(solution)/shard_map/advance/pallas_call | solution.py:457
Async XLA Ops:
  1.9 8.0 %collective-permute-start.1 = (f32[9,8,128]{2,1,0:T(8,128)S(1)}, f32[9,8,128]{2,1,0:T(8,128)S(1)}, u32[]{:S(2)}, u32[]{:S(2)}) collective-permute-start(f32[9,8,128]{2,1,0:T(8,128)S(1)} %get-tuple-element.13), channel_id=1, source_target_pairs={{128,0},{256,128},{384,256},{512,384},{640,512},{768,640},{896,768... | collective-permute-start | bytes 110600 | tf_op jit(solution)/shard_map/ppermute | solution.py:431
  4.0 5.9 %collective-permute-start = (f32[8,8,128]{2,1,0:T(8,128)S(1)}, f32[8,8,128]{2,1,0:T(8,128)S(1)}, u32[]{:S(2)}, u32[]{:S(2)}) collective-permute-start(f32[8,8,128]{2,1,0:T(8,128)S(1)} %get-tuple-element.12), channel_id=1, source_target_pairs={{0,128},{128,256},{256,384},{384,512},{512,640},{640,768},{768,896... | collective-permute-start | bytes 98312 | tf_op jit(solution)/shard_map/ppermute | solution.py:430
  10.0 24.6 %collective-permute-start.3 = (f32[96,128]{1,0:T(8,128)S(1)}, f32[96,128]{1,0:T(8,128)S(1)}, u32[]{:S(2)}, u32[]{:S(2)}) collective-permute-start(f32[96,128]{1,0:T(8,128)S(1)} %get-tuple-element.17), channel_id=1, source_target_pairs={{4,0},{8,4},{12,8},{16,12},{20,16},{24,20},{28,24},{32,28},{36,32}... | collective-permute-start | bytes 147464 | tf_op jit(solution)/shard_map/ppermute | solution.py:441
  27.7 6.9 %collective-permute-start.2 = (f32[88,128]{1,0:T(8,128)S(1)}, f32[88,128]{1,0:T(8,128)S(1)}, u32[]{:S(2)}, u32[]{:S(2)}) collective-permute-start(f32[88,128]{1,0:T(8,128)S(1)} %get-tuple-element.16), channel_id=1, source_target_pairs={{0,4},{4,8},{8,12},{12,16},{16,20},{20,24},{24,28},{28,32},{32,36}... | collective-permute-start | bytes 135176 | tf_op jit(solution)/shard_map/ppermute | solution.py:440

commit v3 on v2

--- a/solution.py
+++ b/solution.py
@@ -20,7 +20,7 @@
 f32 = jnp.float32
 
 
-def gather_block(density, velocity, pressure, field, own, top, bottom, sems):
+def gather_block(density, velocity, pressure, field, corona, own, top, bottom, marks, mask, sems):
     one = pl.ds(0, 1)
     copies = []
     for out, z in ((top, NZ - 1), (bottom, 0)):
@@ -36,12 +36,16 @@
         (velocity, own.at[pl.ds(1, 3)]),
         (pressure, own.at[4]),
         (field, own.at[pl.ds(5, 3)]),
+        (corona, mask),
     ]
     copies = [pltpu.make_async_copy(a, b, sems.at[i]) for i, (a, b) in enumerate(copies)]
     for copy in copies:
         copy.start()
     for copy in copies:
         copy.wait()
+    first, last = lax.axis_index("gz") * NZ, lax.axis_size("gz") * NZ - 1
+    for z in range(ROWS):
+        marks[z] = jnp.full((8, NX), mask[jnp.clip(first + z - 1, 0, last)], jnp.int32)
 
 
 def pack_rows(own, below, above, up, down):
@@ -94,19 +98,14 @@
     return values if by == 0 else pltpu.roll(values, by, axis)
 
 
-def marks_of(corona):
-    first, last = lax.axis_index("gz") * NZ, lax.axis_size("gz") * NZ - 1
-    return [corona[jnp.clip(first + z - 1, 0, last)] for z in range(ROWS)]
-
-
-def cool(corona, ext):
+def cool(marks, ext):
     rho = [ext[0, z] for z in range(ROWS)]
     raw = [ext[4, z] for z in range(ROWS)]
     now = list(raw)
     for _ in range(COOL_STEPS):
-        now = [p / (1.0 + COOL_RATE * jnp.sqrt(r * p)) for r, p in zip(rho, now)]
-    for z, (mark, p, q) in enumerate(zip(marks_of(corona), raw, now)):
-        ext[4, z] = jnp.where(jnp.full((8, NX), mark, jnp.int32) == 1, q, p)
+        now = [p / (1.0 + COOL_RATE * root(r * p)) for r, p in zip(rho, now)]
+    for z, (p, q) in enumerate(zip(raw, now)):
+        ext[4, z] = jnp.where(marks[z] == 1, q, p)
 
 
 def columns_of(ext):
@@ -123,7 +122,7 @@
     return low, high, second
 
 
-def pack_main(corona, own, below, above, ext, cols):
+def pack_main(marks, own, below, above, ext, cols):
     slab_at, slab_count = lax.axis_index("gz"), lax.axis_size("gz")
     for member in range(8):
         for z in Z_MAIN:
@@ -143,7 +142,7 @@
             ext[member, 9] = own[member, NZ - 1]
         ext[5, 10] = own[5, NZ - 1]
 
-    cool(corona, ext)
+    cool(marks, ext)
     for i, v in enumerate(columns_of(ext)):
         cols[i] = v
 
@@ -151,14 +150,14 @@
 PLACES = [(member, z, member * ROWS + z) for member in range(8) for z in range(ROWS)] + [(5, 10, 80)]
 
 
-def pack_edges(corona, main, main_cols, left_rows, right_rows, ext, cols):
+def pack_edges(marks, main, main_cols, left_rows, right_rows, ext, cols):
     row_at, row_count = lax.axis_index("gy"), lax.axis_size("gy")
     for member, z, at in PLACES:
         ext[member, z, 7:8, :] = left_rows[pl.ds(at, 1), :]
         ext[member, z, 0:1, :] = right_rows[pl.ds(at, 1), :]
     for z in range(ROWS):
         ext[6, z, 1:2, :] = right_rows[pl.ds(81 + z, 1), :]
-    cool(corona, ext)
+    cool(marks, ext)
 
     @pl.when(row_at == 0)
     def _():
@@ -187,41 +186,50 @@
         self.sound = GAMMA * p * self.inv
 
 
-def state(cell, normal, axis):
+def root(x):
+    return x * lax.rsqrt(x)
+
+
+def speeds(cell, square, axis):
     b, c = [k for k in range(3) if k != axis]
-    vel, cen = cell.vel, cell.cen
-    across = cen[b] * cen[b] + cen[c] * cen[c]
-    square = normal * normal
-    half = 0.5 * (across + square)
-    total = cell.p + half
-    energy = cell.thermal + half
+    across = cell.cen[b] * cell.cen[b] + cell.cen[c] * cell.cen[c]
     n, t, s = square * cell.inv, across * cell.inv, cell.sound
     gap = s - n - t
-    fast = jnp.sqrt(0.5 * (s + n + t + jnp.sqrt(gap * gap + 4.0 * s * t)))
-    align = vel[axis] * normal + vel[b] * cen[b] + vel[c] * cen[c]
-    va = vel[axis]
-    flux = [cell.mom[axis]]
-    for k in range(3):
-        if k == axis:
-            flux.append(cell.mom[k] * va - square + total)
-        else:
-            flux.append(cell.mom[k] * va - cen[k] * normal)
-    flux.append((energy + total) * va - normal * align)
-    for k in (b, c):
-        flux.append(va * cen[k] - vel[k] * normal)
-    held = [cell.rho] + cell.mom + [energy, cen[b], cen[c]]
-    return va, fast, held, flux
+    inner = root(jnp.maximum(gap * gap + 4.0 * s * t, 1e-30))
+    return across, root(0.5 * (s + n + t + inner))
+
+
+def side(cell, normal, square, across, axis, speed, weight, member):
+    vel, cen, va = cell.vel, cell.cen, cell.vel[axis]
+    w, wn = weight * (va - speed), weight * normal
+    if member == 0:
+        return cell.rho * w
+    if member == axis + 1:
+        return cell.mom[axis] * w + weight * (cell.p + 0.5 * (across - square))
+    if member < 4:
+        return cell.mom[member - 1] * w - cen[member - 1] * wn
+    b, c = [k for k in range(3) if k != axis]
+    if member == 4:
+        half = 0.5 * (across + square)
+        align = va * normal + vel[b] * cen[b] + vel[c] * cen[c]
+        return (cell.thermal + half) * w + weight * ((cell.p + half) * va - normal * align)
+    k = (b, c)[member - 5]
+    return cen[k] * w - vel[k] * wn
 
 
 def hll(lower, upper, normal, axis, members):
-    lv, lf, lu, lflux = state(lower, normal, axis)
-    uv, uf, uu, uflux = state(upper, normal, axis)
+    square = normal * normal
+    la, lf = speeds(lower, square, axis)
+    ua, uf = speeds(upper, square, axis)
+    lv, uv = lower.vel[axis], upper.vel[axis]
     slow = jnp.minimum(jnp.minimum(lv - lf, uv - uf), 0.0)
     fast = jnp.maximum(jnp.maximum(lv + lf, uv + uf), 0.0)
     inverse = 1.0 / (fast - slow)
     a, b = fast * inverse, slow * inverse
-    c = slow * a
-    return {m: a * lflux[m] - b * uflux[m] + c * (uu[m] - lu[m]) for m in members}
+    return {
+        m: side(lower, normal, square, la, axis, slow, a, m) - side(upper, normal, square, ua, axis, fast, b, m)
+        for m in members
+    }
 
 
 def member_of(axis, component):
@@ -397,15 +405,14 @@
 
 
 VMEM = pl.BlockSpec(memory_space=pltpu.VMEM)
-SMEM = pl.BlockSpec(memory_space=pltpu.SMEM)
 
 
 def shape(*dims):
     return jax.ShapeDtypeStruct(dims, f32)
 
 
-def held(*dims):
-    return pltpu.VMEM(dims, f32)
+def held(*dims, dtype=f32):
+    return pltpu.VMEM(dims, dtype)
 
 
 def near(*arrays):
@@ -418,14 +425,14 @@
 
 
 def on_device(density, velocity, pressure, field, corona):
-    own, top, bottom = pl.pallas_call(
+    own, top, bottom, marks = pl.pallas_call(
         gather_block,
-        out_shape=(held(8, NZ, NY, NX), held(8, NY, NX), held(9, NY, NX)),
-        in_specs=[pl.BlockSpec(memory_space=pl.ANY)] * 4,
-        out_specs=(VMEM,) * 3,
-        scratch_shapes=[pltpu.SemaphoreType.DMA((13,))],
+        out_shape=(held(8, NZ, NY, NX), held(8, NY, NX), held(9, NY, NX), held(ROWS, NY, NX, dtype=jnp.int32)),
+        in_specs=[pl.BlockSpec(memory_space=pl.ANY)] * 5,
+        out_specs=(VMEM,) * 4,
+        scratch_shapes=[pltpu.SMEM(corona.shape, jnp.int32), pltpu.SemaphoreType.DMA((14,))],
         name="gather_block",
-    )(density, velocity, pressure, field)
+    )(density, velocity, pressure, field, corona)
     up, down = neighbours("gz")
     below = lax.ppermute(top, "gz", up)
     above = lax.ppermute(bottom, "gz", down)
@@ -442,17 +449,17 @@
     main, main_cols = pl.pallas_call(
         pack_main,
         out_shape=(held(8, 11, 8, NX), held(3, 8, NX)),
-        in_specs=[SMEM] + [VMEM] * 3,
+        in_specs=[VMEM] * 4,
         out_specs=(VMEM, VMEM),
         name="pack_main",
-    )(corona, *near(own, below, above))
+    )(*near(marks, own, below, above))
     edges, cols = pl.pallas_call(
         pack_edges,
         out_shape=(held(8, 11, 8, NX), held(3, 16, NX)),
-        in_specs=[SMEM] + [VMEM] * 4,
+        in_specs=[VMEM] * 5,
         out_specs=(VMEM, VMEM),
         name="pack_edges",
-    )(corona, *near(main, main_cols, left_rows, right_rows))
+    )(*near(marks, main, main_cols, left_rows, right_rows))
     gathered = lax.all_gather(cols, "gx", axis=0)
     return pl.pallas_call(
         advance,

time: 51 us -> 50.2 us (0.984)
  Pallas kernels: 5.8 us -> 4.33 us
  waiting for transfers between devices: 6.76 us -> 7.43 us
    pallas_call x1, Pallas kernels: 1.13 us -> 0.45 us  [on_device(): pl.pallas_call(pack_edges, out_shape=(held(8, 11, 8, NX), held(3, 16, NX)...]
    ppermute x1, waiting for transfers between devices: 4.01 us -> 4.68 us  [on_device(): left_rows = lax.ppermute(rows_up, 'gy', up)]
    pallas_call x1, Pallas kernels: 0.96 us -> 0.29 us  [on_device(): pl.pallas_call(pack_main, out_shape=(held(8, 11, 8, NX), held(3, 8, NX)),...]
  transfers between devices with their start and end apart: 4 -> 4, of which waited for: 2 -> 2; matrix products, arithmetic and copies ran while one was open for 0% -> 0% of each run, Pallas kernels for 2% -> 1%
where the time goes in v3:
time: 50.2 us; the launch traced here: 50 us
  starting transfers between devices  24.9 us (50%)
  blocking collectives  12.6 us (25%)
  waiting for transfers between devices  7.43 us (15%)
  Pallas kernels  4.33 us (9%)
  between operations  0.69 us (1%)
    ppermute x1, starting transfers between devices, on_device(): right_rows = lax.ppermute(rows_down, 'gy', down)  17.7 us
    all_gather x1, blocking collectives, on_device(): gathered = lax.all_gather(cols, 'gx', axis=0)  12.6 us
    ppermute x1, waiting for transfers between devices, on_device(): left_rows = lax.ppermute(rows_up, 'gy', up)  4.68 us
    ppermute x1, starting transfers between devices, on_device(): below = lax.ppermute(top, 'gz', up)  3.12 us
    ppermute x1, waiting for transfers between devices, on_device(): below = lax.ppermute(top, 'gz', up)  2.74 us
    pallas_call x1, Pallas kernels, on_device(): pl.pallas_call(advance, out_shape=(shape(5, NZ, NY, NX), shape(3, NZ, NY,...  2.25 us
    ppermute x1, starting transfers between devices, on_device(): above = lax.ppermute(bottom, 'gz', down)  2.16 us
    ppermute x1, starting transfers between devices, on_device(): left_rows = lax.ppermute(rows_up, 'gy', up)  1.92 us
  transfers between devices with their start and end apart: 4, of which 2 were waited for; matrix products, arithmetic and copies ran while one was open for 0% of the time, Pallas kernels for 1%

profile of v3, /device:TPU:121, one launch (start us, length us, event | category | flops | bytes accessed | tf_op | source)
XLA Modules:
  0.0 50.0 jit_solution(1945757104386703635)
XLA Ops:
  0.6 1.3 %gather_block.1 = (f32[8,8,8,128]{3,2,1,0:T(8,128)S(1)}, f32[8,8,128]{2,1,0:T(8,128)S(1)}, f32[9,8,128]{2,1,0:T(8,128)S(1)}, s32[10,8,128]{2,1,0:T(8,128)S(1)}) custom-call(f32[8,8,128]{2,1,0:T(8,128)} %density.1, f32[3,8,8,128]{3,2,1,0:T(8,128)} %velocity.1, f32[8,8,128]{2,1,0:T(8,128)} %pressure.1, f32[3,8,8,128]{3,2,1,0:T(8,128)} %field.1, s32[64]{0:T(128)} %corona.1), custom_call_target="tpu_custom_call" | custom-call | tf_op jit(solution)/shard_map/gather_block/pallas_call | solution.py:428
  1.9 2.2 %collective-permute-start.1 = (f32[9,8,128]{2,1,0:T(8,128)S(1)}, f32[9,8,128]{2,1,0:T(8,128)S(1)}, u32[]{:S(2)}, u32[]{:S(2)}) collective-permute-start(f32[9,8,128]{2,1,0:T(8,128)S(1)} %get-tuple-element.15), channel_id=1, source_target_pairs={{128,0},{256,128},{384,256},{512,384},{640,512},{768,640},{896,768... | collective-permute-start | bytes 110600 | tf_op jit(solution)/shard_map/ppermute | solution.py:438
  4.1 3.1 %collective-permute-start = (f32[8,8,128]{2,1,0:T(8,128)S(1)}, f32[8,8,128]{2,1,0:T(8,128)S(1)}, u32[]{:S(2)}, u32[]{:S(2)}) collective-permute-start(f32[8,8,128]{2,1,0:T(8,128)S(1)} %get-tuple-element.14), channel_id=1, source_target_pairs={{0,128},{128,256},{256,384},{384,512},{512,640},{640,768},{768,896... | collective-permute-start | bytes 98312 | tf_op jit(solution)/shard_map/ppermute | solution.py:437
  7.2 2.7 %collective-permute-done.below = f32[8,8,128]{2,1,0:T(8,128)S(1)} collective-permute-done((f32[8,8,128]{2,1,0:T(8,128)S(1)}, f32[8,8,128]{2,1,0:T(8,128)S(1)}, u32[]{:S(2)}, u32[]{:S(2)}) %collective-permute-start) | collective-permute-done | bytes 32800 | tf_op jit(solution)/shard_map/ppermute | solution.py:437
  9.9 0.0 collective-permute-done.1.above
  10.0 0.1 pack_rows.1
  10.0 17.7 %collective-permute-start.3 = (f32[96,128]{1,0:T(8,128)S(1)}, f32[96,128]{1,0:T(8,128)S(1)}, u32[]{:S(2)}, u32[]{:S(2)}) collective-permute-start(f32[96,128]{1,0:T(8,128)S(1)} %get-tuple-element.19), channel_id=1, source_target_pairs={{4,0},{8,4},{12,8},{16,12},{20,16},{24,20},{28,24},{32,28},{36,32}... | collective-permute-start | bytes 147464 | tf_op jit(solution)/shard_map/ppermute | solution.py:448
  27.7 1.9 %collective-permute-start.2 = (f32[88,128]{1,0:T(8,128)S(1)}, f32[88,128]{1,0:T(8,128)S(1)}, u32[]{:S(2)}, u32[]{:S(2)}) collective-permute-start(f32[88,128]{1,0:T(8,128)S(1)} %get-tuple-element.18), channel_id=1, source_target_pairs={{0,4},{4,8},{8,12},{12,16},{16,20},{20,24},{24,28},{28,32},{32,36}... | collective-permute-start | bytes 135176 | tf_op jit(solution)/shard_map/ppermute | solution.py:447
  29.7 0.3 pack_main.1
  30.0 4.7 %collective-permute-done.2.left_rows = f32[88,128]{1,0:T(8,128)S(1)} collective-permute-done((f32[88,128]{1,0:T(8,128)S(1)}, f32[88,128]{1,0:T(8,128)S(1)}, u32[]{:S(2)}, u32[]{:S(2)}) %collective-permute-start.2) | collective-permute-done | bytes 45088 | tf_op jit(solution)/shard_map/ppermute | solution.py:447
  34.6 0.0 collective-permute-done.3.right_rows
  34.6 0.5 pack_edges.1
  35.1 12.6 %all-gather = f32[12,16,128]{2,1,0:T(8,128)S(1)} all-gather(f32[3,16,128]{2,1,0:T(8,128)S(1)} %get-tuple-element.20.own_cols), channel_id=2, replica_groups=mesh['gz'=8,'gy'=32,'gx'=4] {'gx'}, dimensions={0}, use_global_device_ids=true | all-gather | bytes 122880 | tf_op jit(solution)/shard_map/all_gather | solution.py:463
  47.7 2.3 %advance.1 = (f32[5,8,8,128]{3,2,1,0:T(8,128)}, f32[3,8,8,128]{3,2,1,0:T(8,128)}) custom-call(f32[4,3,16,128]{3,2,1,0:T(8,128)S(1)} %bitcast.1, f32[3,16,128]{2,1,0:T(8,128)S(1)} %get-tuple-element.20.own_cols, f32[8,11,8,128]{3,2,1,0:T(8,128)S(1)} %get-tuple-element.16.main, f32[8,11,8,128]{3,2,1,0:T(8,128)S(1)} %get-tuple-element.21.edges), custom_call_target="tpu_custom_call" | custom-call | tf_op jit(solution)/shard_map/advance/pallas_call | solution.py:464
Async XLA Ops:
  1.9 8.0 %collective-permute-start.1 = (f32[9,8,128]{2,1,0:T(8,128)S(1)}, f32[9,8,128]{2,1,0:T(8,128)S(1)}, u32[]{:S(2)}, u32[]{:S(2)}) collective-permute-start(f32[9,8,128]{2,1,0:T(8,128)S(1)} %get-tuple-element.15), channel_id=1, source_target_pairs={{128,0},{256,128},{384,256},{512,384},{640,512},{768,640},{896,768... | collective-permute-start | bytes 110600 | tf_op jit(solution)/shard_map/ppermute | solution.py:438
  4.1 5.9 %collective-permute-start = (f32[8,8,128]{2,1,0:T(8,128)S(1)}, f32[8,8,128]{2,1,0:T(8,128)S(1)}, u32[]{:S(2)}, u32[]{:S(2)}) collective-permute-start(f32[8,8,128]{2,1,0:T(8,128)S(1)} %get-tuple-element.14), channel_id=1, source_target_pairs={{0,128},{128,256},{256,384},{384,512},{512,640},{640,768},{768,896... | collective-permute-start | bytes 98312 | tf_op jit(solution)/shard_map/ppermute | solution.py:437
  10.0 24.6 %collective-permute-start.3 = (f32[96,128]{1,0:T(8,128)S(1)}, f32[96,128]{1,0:T(8,128)S(1)}, u32[]{:S(2)}, u32[]{:S(2)}) collective-permute-start(f32[96,128]{1,0:T(8,128)S(1)} %get-tuple-element.19), channel_id=1, source_target_pairs={{4,0},{8,4},{12,8},{16,12},{20,16},{24,20},{28,24},{32,28},{36,32}... | collective-permute-start | bytes 147464 | tf_op jit(solution)/shard_map/ppermute | solution.py:448
  27.7 6.9 %collective-permute-start.2 = (f32[88,128]{1,0:T(8,128)S(1)}, f32[88,128]{1,0:T(8,128)S(1)}, u32[]{:S(2)}, u32[]{:S(2)}) collective-permute-start(f32[88,128]{1,0:T(8,128)S(1)} %get-tuple-element.18), channel_id=1, source_target_pairs={{0,4},{4,8},{8,12},{12,16},{16,20},{20,24},{24,28},{28,32},{32,36}... | collective-permute-start | bytes 135176 | tf_op jit(solution)/shard_map/ppermute | solution.py:447

commit v4 on v3

--- a/solution.py
+++ b/solution.py
@@ -20,29 +20,36 @@
 f32 = jnp.float32
 
 
-def gather_block(density, velocity, pressure, field, corona, own, top, bottom, marks, mask, sems):
+def run_copies(pairs, sems):
+    copies = [pltpu.make_async_copy(a, b, sems.at[i]) for i, (a, b) in enumerate(pairs)]
+    for copy in copies:
+        copy.start()
+    for copy in copies:
+        copy.wait()
+
+
+def gather_layers(density, velocity, pressure, field, top, bottom, sems):
     one = pl.ds(0, 1)
-    copies = []
+    pairs = [(field.at[0, pl.ds(1, 1)], bottom.at[pl.ds(8, 1)])]
     for out, z in ((top, NZ - 1), (bottom, 0)):
-        copies += [
+        pairs += [
             (density.at[pl.ds(z, 1)], out.at[one]),
             (velocity.at[:, z], out.at[pl.ds(1, 3)]),
             (pressure.at[pl.ds(z, 1)], out.at[pl.ds(4, 1)]),
             (field.at[:, z], out.at[pl.ds(5, 3)]),
         ]
-    copies += [
-        (field.at[0, pl.ds(1, 1)], bottom.at[pl.ds(8, 1)]),
+    run_copies(pairs, sems)
+
+
+def gather_block(density, velocity, pressure, field, corona, own, marks, mask, sems):
+    pairs = [
         (density, own.at[0]),
         (velocity, own.at[pl.ds(1, 3)]),
         (pressure, own.at[4]),
         (field, own.at[pl.ds(5, 3)]),
         (corona, mask),
     ]
-    copies = [pltpu.make_async_copy(a, b, sems.at[i]) for i, (a, b) in enumerate(copies)]
-    for copy in copies:
-        copy.start()
-    for copy in copies:
-        copy.wait()
+    run_copies(pairs, sems)
     first, last = lax.axis_index("gz") * NZ, lax.axis_size("gz") * NZ - 1
     for z in range(ROWS):
         marks[z] = jnp.full((8, NX), mask[jnp.clip(first + z - 1, 0, last)], jnp.int32)
@@ -425,17 +432,26 @@
 
 
 def on_device(density, velocity, pressure, field, corona):
-    own, top, bottom, marks = pl.pallas_call(
-        gather_block,
-        out_shape=(held(8, NZ, NY, NX), held(8, NY, NX), held(9, NY, NX), held(ROWS, NY, NX, dtype=jnp.int32)),
-        in_specs=[pl.BlockSpec(memory_space=pl.ANY)] * 5,
-        out_specs=(VMEM,) * 4,
-        scratch_shapes=[pltpu.SMEM(corona.shape, jnp.int32), pltpu.SemaphoreType.DMA((14,))],
-        name="gather_block",
-    )(density, velocity, pressure, field, corona)
+    anywhere = pl.BlockSpec(memory_space=pl.ANY)
+    top, bottom = pl.pallas_call(
+        gather_layers,
+        out_shape=(held(8, NY, NX), held(9, NY, NX)),
+        in_specs=[anywhere] * 4,
+        out_specs=(VMEM,) * 2,
+        scratch_shapes=[pltpu.SemaphoreType.DMA((9,))],
+        name="gather_layers",
+    )(density, velocity, pressure, field)
     up, down = neighbours("gz")
     below = lax.ppermute(top, "gz", up)
     above = lax.ppermute(bottom, "gz", down)
+    own, marks = pl.pallas_call(
+        gather_block,
+        out_shape=(held(8, NZ, NY, NX), held(ROWS, NY, NX, dtype=jnp.int32)),
+        in_specs=[anywhere] * 5,
+        out_specs=(VMEM,) * 2,
+        scratch_shapes=[pltpu.SMEM(corona.shape, jnp.int32), pltpu.SemaphoreType.DMA((5,))],
+        name="gather_block",
+    )(density, velocity, pressure, field, corona)
     rows_up, rows_down = pl.pallas_call(
         pack_rows,
         out_shape=(held(UP_ROWS, NX), held(DOWN_ROWS, NX)),

time: 50.2 us -> 49.9 us (level)
  waiting for transfers between devices: 7.43 us -> 6.35 us
  Pallas kernels: 4.33 us -> 5.05 us
    ppermute x1, waiting for transfers between devices: 2.74 us -> 1.67 us  [on_device(): below = lax.ppermute(top, 'gz', up)]
    pallas_call x1 -> x2, Pallas kernels: 1.27 us -> 1.99 us  [the longest x1 1.07 us: on_device(): pl.pallas_call(gather_block, out_shape=(held(8, NZ, NY, NX), held(ROWS, N...]
  transfers between devices with their start and end apart: 4 -> 4, of which waited for: 2 -> 2; matrix products, arithmetic and copies ran while one was open for 0% -> 0% of each run, Pallas kernels for 1% -> 3%
where the time goes in v4:
time: 49.9 us; the launch traced here: 49.6 us
  starting transfers between devices  24.9 us (50%)
  blocking collectives  12.6 us (25%)
  waiting for transfers between devices  6.35 us (13%)
  Pallas kernels  5.05 us (10%)
  between operations  0.69 us (1%)
    ppermute x1, starting transfers between devices, on_device(): right_rows = lax.ppermute(rows_down, 'gy', down)  17.7 us
    all_gather x1, blocking collectives, on_device(): gathered = lax.all_gather(cols, 'gx', axis=0)  12.6 us
    ppermute x1, waiting for transfers between devices, on_device(): left_rows = lax.ppermute(rows_up, 'gy', up)  4.68 us
    ppermute x1, starting transfers between devices, on_device(): below = lax.ppermute(top, 'gz', up)  3.12 us
    pallas_call x1, Pallas kernels, on_device(): pl.pallas_call(advance, out_shape=(shape(5, NZ, NY, NX), shape(3, NZ, NY,...  2.25 us
    ppermute x1, starting transfers between devices, on_device(): above = lax.ppermute(bottom, 'gz', down)  2.16 us
    ppermute x1, starting transfers between devices, on_device(): left_rows = lax.ppermute(rows_up, 'gy', up)  1.92 us
    ppermute x1, waiting for transfers between devices, on_device(): below = lax.ppermute(top, 'gz', up)  1.67 us
  transfers between devices with their start and end apart: 4, of which 2 were waited for; matrix products, arithmetic and copies ran while one was open for 0% of the time, Pallas kernels for 3%

profile of v4, /device:TPU:121, one launch (start us, length us, event | category | flops | bytes accessed | tf_op | source)
XLA Modules:
  0.0 49.6 jit_solution(8542883448557281023)
XLA Ops:
  0.6 0.9 %gather_layers.1 = (f32[8,8,128]{2,1,0:T(8,128)S(1)}, f32[9,8,128]{2,1,0:T(8,128)S(1)}) custom-call(f32[8,8,128]{2,1,0:T(8,128)} %density.3, f32[3,8,8,128]{3,2,1,0:T(8,128)} %velocity.3, f32[8,8,128]{2,1,0:T(8,128)} %pressure.3, f32[3,8,8,128]{3,2,1,0:T(8,128)} %field.3), custom_call_target="tpu_custom_call" | custom-call | tf_op jit(solution)/shard_map/gather_layers/pallas_call | solution.py:436
  1.6 2.2 %collective-permute-start.1 = (f32[9,8,128]{2,1,0:T(8,128)S(1)}, f32[9,8,128]{2,1,0:T(8,128)S(1)}, u32[]{:S(2)}, u32[]{:S(2)}) collective-permute-start(f32[9,8,128]{2,1,0:T(8,128)S(1)} %get-tuple-element.15), channel_id=1, source_target_pairs={{128,0},{256,128},{384,256},{512,384},{640,512},{768,640},{896,768... | collective-permute-start | bytes 110600 | tf_op jit(solution)/shard_map/ppermute | solution.py:446
  3.7 3.1 %collective-permute-start = (f32[8,8,128]{2,1,0:T(8,128)S(1)}, f32[8,8,128]{2,1,0:T(8,128)S(1)}, u32[]{:S(2)}, u32[]{:S(2)}) collective-permute-start(f32[8,8,128]{2,1,0:T(8,128)S(1)} %get-tuple-element.14), channel_id=1, source_target_pairs={{0,128},{128,256},{256,384},{384,512},{512,640},{640,768},{768,896... | collective-permute-start | bytes 98312 | tf_op jit(solution)/shard_map/ppermute | solution.py:445
  6.9 1.1 %gather_block.1 = (f32[8,8,8,128]{3,2,1,0:T(8,128)S(1)}, s32[10,8,128]{2,1,0:T(8,128)S(1)}) custom-call(f32[8,8,128]{2,1,0:T(8,128)} %density.3, f32[3,8,8,128]{3,2,1,0:T(8,128)} %velocity.3, f32[8,8,128]{2,1,0:T(8,128)} %pressure.3, f32[3,8,8,128]{3,2,1,0:T(8,128)} %field.3, s32[64]{0:T(128)} %corona.1), custom_call_target="tpu_custom_call" | custom-call | tf_op jit(solution)/shard_map/gather_block/pallas_call | solution.py:447
  7.9 1.7 %collective-permute-done.below = f32[8,8,128]{2,1,0:T(8,128)S(1)} collective-permute-done((f32[8,8,128]{2,1,0:T(8,128)S(1)}, f32[8,8,128]{2,1,0:T(8,128)S(1)}, u32[]{:S(2)}, u32[]{:S(2)}) %collective-permute-start) | collective-permute-done | bytes 32800 | tf_op jit(solution)/shard_map/ppermute | solution.py:445
  9.6 0.0 collective-permute-done.1.above
  9.6 0.1 pack_rows.1
  9.7 17.7 %collective-permute-start.3 = (f32[96,128]{1,0:T(8,128)S(1)}, f32[96,128]{1,0:T(8,128)S(1)}, u32[]{:S(2)}, u32[]{:S(2)}) collective-permute-start(f32[96,128]{1,0:T(8,128)S(1)} %get-tuple-element.19), channel_id=1, source_target_pairs={{4,0},{8,4},{12,8},{16,12},{20,16},{24,20},{28,24},{32,28},{36,32}... | collective-permute-start | bytes 147464 | tf_op jit(solution)/shard_map/ppermute | solution.py:464
  27.4 1.9 %collective-permute-start.2 = (f32[88,128]{1,0:T(8,128)S(1)}, f32[88,128]{1,0:T(8,128)S(1)}, u32[]{:S(2)}, u32[]{:S(2)}) collective-permute-start(f32[88,128]{1,0:T(8,128)S(1)} %get-tuple-element.18), channel_id=1, source_target_pairs={{0,4},{4,8},{8,12},{12,16},{16,20},{20,24},{24,28},{28,32},{32,36}... | collective-permute-start | bytes 135176 | tf_op jit(solution)/shard_map/ppermute | solution.py:463
  29.3 0.3 pack_main.1
  29.6 4.7 %collective-permute-done.2.left_rows = f32[88,128]{1,0:T(8,128)S(1)} collective-permute-done((f32[88,128]{1,0:T(8,128)S(1)}, f32[88,128]{1,0:T(8,128)S(1)}, u32[]{:S(2)}, u32[]{:S(2)}) %collective-permute-start.2) | collective-permute-done | bytes 45088 | tf_op jit(solution)/shard_map/ppermute | solution.py:463
  34.3 0.0 collective-permute-done.3.right_rows
  34.3 0.5 pack_edges.1
  34.8 12.6 %all-gather = f32[12,16,128]{2,1,0:T(8,128)S(1)} all-gather(f32[3,16,128]{2,1,0:T(8,128)S(1)} %get-tuple-element.20.own_cols), channel_id=2, replica_groups=mesh['gz'=8,'gy'=32,'gx'=4] {'gx'}, dimensions={0}, use_global_device_ids=true | all-gather | bytes 122880 | tf_op jit(solution)/shard_map/all_gather | solution.py:479
  47.4 2.3 %advance.1 = (f32[5,8,8,128]{3,2,1,0:T(8,128)}, f32[3,8,8,128]{3,2,1,0:T(8,128)}) custom-call(f32[4,3,16,128]{3,2,1,0:T(8,128)S(1)} %bitcast.1, f32[3,16,128]{2,1,0:T(8,128)S(1)} %get-tuple-element.20.own_cols, f32[8,11,8,128]{3,2,1,0:T(8,128)S(1)} %get-tuple-element.16.main, f32[8,11,8,128]{3,2,1,0:T(8,128)S(1)} %get-tuple-element.21.edges), custom_call_target="tpu_custom_call" | custom-call | tf_op jit(solution)/shard_map/advance/pallas_call | solution.py:480
Async XLA Ops:
  1.6 8.0 %collective-permute-start.1 = (f32[9,8,128]{2,1,0:T(8,128)S(1)}, f32[9,8,128]{2,1,0:T(8,128)S(1)}, u32[]{:S(2)}, u32[]{:S(2)}) collective-permute-start(f32[9,8,128]{2,1,0:T(8,128)S(1)} %get-tuple-element.15), channel_id=1, source_target_pairs={{128,0},{256,128},{384,256},{512,384},{640,512},{768,640},{896,768... | collective-permute-start | bytes 110600 | tf_op jit(solution)/shard_map/ppermute | solution.py:446
  3.7 5.9 %collective-permute-start = (f32[8,8,128]{2,1,0:T(8,128)S(1)}, f32[8,8,128]{2,1,0:T(8,128)S(1)}, u32[]{:S(2)}, u32[]{:S(2)}) collective-permute-start(f32[8,8,128]{2,1,0:T(8,128)S(1)} %get-tuple-element.14), channel_id=1, source_target_pairs={{0,128},{128,256},{256,384},{384,512},{512,640},{640,768},{768,896... | collective-permute-start | bytes 98312 | tf_op jit(solution)/shard_map/ppermute | solution.py:445
  9.7 24.6 %collective-permute-start.3 = (f32[96,128]{1,0:T(8,128)S(1)}, f32[96,128]{1,0:T(8,128)S(1)}, u32[]{:S(2)}, u32[]{:S(2)}) collective-permute-start(f32[96,128]{1,0:T(8,128)S(1)} %get-tuple-element.19), channel_id=1, source_target_pairs={{4,0},{8,4},{12,8},{16,12},{20,16},{24,20},{28,24},{32,28},{36,32}... | collective-permute-start | bytes 147464 | tf_op jit(solution)/shard_map/ppermute | solution.py:464
  27.4 6.9 %collective-permute-start.2 = (f32[88,128]{1,0:T(8,128)S(1)}, f32[88,128]{1,0:T(8,128)S(1)}, u32[]{:S(2)}, u32[]{:S(2)}) collective-permute-start(f32[88,128]{1,0:T(8,128)S(1)} %get-tuple-element.18), channel_id=1, source_target_pairs={{0,4},{4,8},{8,12},{12,16},{16,20},{20,24},{24,28},{28,32},{32,36}... | collective-permute-start | bytes 135176 | tf_op jit(solution)/shard_map/ppermute | solution.py:463

commit v5 on v4

--- a/solution.py
+++ b/solution.py
@@ -157,7 +157,7 @@
 PLACES = [(member, z, member * ROWS + z) for member in range(8) for z in range(ROWS)] + [(5, 10, 80)]
 
 
-def pack_edges(marks, main, main_cols, left_rows, right_rows, ext, cols):
+def pack_edges(marks, main, main_cols, left_rows, right_rows, ext, cols, near_out, far_out):
     row_at, row_count = lax.axis_index("gy"), lax.axis_size("gy")
     for member, z, at in PLACES:
         ext[member, z, 7:8, :] = left_rows[pl.ds(at, 1), :]
@@ -181,6 +181,17 @@
     for i, v in enumerate(columns_of(ext)):
         cols[i, 0:8, :] = main_cols[i]
         cols[i, 8:16, :] = v
+    even = lax.rem(lax.axis_index("gx"), 2) == 0
+
+    @pl.when(even)
+    def _():
+        near_out[0], near_out[1] = cols[1], cols[2]
+        far_out[0], far_out[1] = cols[0], cols[2]
+
+    @pl.when(jnp.logical_not(even))
+    def _():
+        near_out[0], near_out[1] = cols[0], cols[2]
+        far_out[0], far_out[1] = cols[1], cols[2]
 
 
 class Cell:
@@ -243,11 +254,9 @@
     return 5 + [k for k in range(3) if k != axis].index(component)
 
 
-def advance(gathered, own_cols, main, edges, conserved_out, faces_out, conserved, faces_new, sems):
+def advance(near_in, far_in, own_cols, main, edges, conserved_out, faces_out, conserved, faces_new, sems):
     lane, sub = lanes(), sublanes()
-    size = lax.axis_size("gx")
-    at = lax.axis_index("gx")
-    left, right = lax.rem(at + size - 1, size), lax.rem(at + 1, size)
+    even = jnp.full((8, NX), lax.rem(lax.axis_index("gx"), 2), jnp.int32) == 0
     first_lane, last_lane = lane == 0, lane == NX - 1
     first_row, last_row = sub == 0, sub == 7
     slot = lane % 8
@@ -266,9 +275,11 @@
     def up_x(q, side, source):
         return jnp.where(last_lane, roll(side, NX - 1 - source, 1), roll(q, -1, 1))
 
-    low_r = [gathered[right, 0, 8 * t : 8 * t + 8, :] for t in range(2)]
-    two_r = [gathered[right, 2, 8 * t : 8 * t + 8, :] for t in range(2)]
-    high_l = [gathered[left, 1, 8 * t : 8 * t + 8, :] for t in range(2)]
+    got = lambda side, i: [side[i, 8 * t : 8 * t + 8, :] for t in range(2)]
+    pick = lambda p, q: [jnp.where(even, v, w) for v, w in zip(p, q)]
+    low_r = pick(got(near_in, 0), got(far_in, 0))
+    two_r = pick(got(near_in, 1), got(far_in, 1))
+    high_l = pick(got(far_in, 0), got(near_in, 0))
     own_low = [own_cols[0, 8 * t : 8 * t + 8, :] for t in range(2)]
     own_high = [own_cols[1, 8 * t : 8 * t + 8, :] for t in range(2)]
 
@@ -469,18 +480,22 @@
         out_specs=(VMEM, VMEM),
         name="pack_main",
     )(*near(marks, own, below, above))
-    edges, cols = pl.pallas_call(
+    edges, cols, to_near, to_far = pl.pallas_call(
         pack_edges,
-        out_shape=(held(8, 11, 8, NX), held(3, 16, NX)),
+        out_shape=(held(8, 11, 8, NX), held(3, 16, NX), held(2, 16, NX), held(2, 16, NX)),
         in_specs=[VMEM] * 5,
-        out_specs=(VMEM, VMEM),
+        out_specs=(VMEM,) * 4,
         name="pack_edges",
     )(*near(marks, main, main_cols, left_rows, right_rows))
-    gathered = lax.all_gather(cols, "gx", axis=0)
+    count = lax.axis_size("gx")
+    near_pairs = [(i, i ^ 1) for i in range(count)]
+    far_pairs = [p for i in range(1, count, 2) for p in ((i, (i + 1) % count), ((i + 1) % count, i))]
+    from_far = lax.ppermute(to_far, "gx", far_pairs)
+    from_near = lax.ppermute(to_near, "gx", near_pairs)
     return pl.pallas_call(
         advance,
         out_shape=(shape(5, NZ, NY, NX), shape(3, NZ, NY, NX)),
-        in_specs=[VMEM] * 4,
+        in_specs=[VMEM] * 5,
         out_specs=(pl.BlockSpec(memory_space=pl.ANY),) * 2,
         scratch_shapes=[
             pltpu.VMEM((5, NZ, NY, NX), f32),
@@ -488,7 +503,7 @@
             pltpu.SemaphoreType.DMA((2 * NZ,)),
         ],
         name="advance",
-    )(*near(gathered, cols, main, edges))
+    )(*near(from_near, from_far, cols, main, edges))
 
 
 def solution(mesh):

time: 49.9 us -> 51.8 us (1.038)
  blocking collectives: 12.6 us -> 0 us
  starting transfers between devices: 24.9 us -> 33.3 us
  waiting for transfers between devices: 6.35 us -> 12.3 us
    all_gather x1 -> x0, blocking collectives: 12.6 us -> none  [on_device(): gathered = lax.all_gather(cols, 'gx', axis=0)]
    ppermute x0 -> x2, starting transfers between devices: none -> 8.42 us  [the longest x1 5.45 us: on_device(): from_near = lax.ppermute(to_near, 'gx', near_pairs)]
    ppermute x0 -> x2, waiting for transfers between devices: none -> 5.97 us  [the longest x1 5.97 us: on_device(): from_far = lax.ppermute(to_far, 'gx', far_pairs)]
  transfers between devices with their start and end apart: 4 -> 6, of which waited for: 2 -> 3; matrix products, arithmetic and copies ran while one was open for 0% -> 0% of each run, Pallas kernels for 3% -> 3%
where the time goes in v5:
time: 51.8 us; the launch traced here: 51.4 us
  starting transfers between devices  33.3 us (64%)
  waiting for transfers between devices  12.3 us (24%)
  Pallas kernels  5.05 us (10%)
  between operations  0.72 us (1%)
    ppermute x1, starting transfers between devices, on_device(): right_rows = lax.ppermute(rows_down, 'gy', down)  17.7 us
    ppermute x1, waiting for transfers between devices, on_device(): from_far = lax.ppermute(to_far, 'gx', far_pairs)  5.97 us
    ppermute x1, starting transfers between devices, on_device(): from_near = lax.ppermute(to_near, 'gx', near_pairs)  5.45 us
    ppermute x1, waiting for transfers between devices, on_device(): left_rows = lax.ppermute(rows_up, 'gy', up)  4.68 us
    ppermute x1, starting transfers between devices, on_device(): below = lax.ppermute(top, 'gz', up)  3.12 us
    ppermute x1, starting transfers between devices, on_device(): from_far = lax.ppermute(to_far, 'gx', far_pairs)  2.98 us
    pallas_call x1, Pallas kernels, on_device(): pl.pallas_call(advance, out_shape=(shape(5, NZ, NY, NX), shape(3, NZ, NY,...  2.25 us
    ppermute x1, starting transfers between devices, on_device(): above = lax.ppermute(bottom, 'gz', down)  2.16 us
  transfers between devices with their start and end apart: 6, of which 3 were waited for; matrix products, arithmetic and copies ran while one was open for 0% of the time, Pallas kernels for 3%

profile of v5, /device:TPU:121, one launch (start us, length us, event | category | flops | bytes accessed | tf_op | source)
XLA Modules:
  0.0 51.4 jit_solution(9769107304489155601)
XLA Ops:
  0.6 0.9 %gather_layers.1 = (f32[8,8,128]{2,1,0:T(8,128)S(1)}, f32[9,8,128]{2,1,0:T(8,128)S(1)}) custom-call(f32[8,8,128]{2,1,0:T(8,128)} %density.3, f32[3,8,8,128]{3,2,1,0:T(8,128)} %velocity.3, f32[8,8,128]{2,1,0:T(8,128)} %pressure.3, f32[3,8,8,128]{3,2,1,0:T(8,128)} %field.3), custom_call_target="tpu_custom_call" | custom-call | tf_op jit(solution)/shard_map/gather_layers/pallas_call | solution.py:447
  1.6 2.2 %collective-permute-start.1 = (f32[9,8,128]{2,1,0:T(8,128)S(1)}, f32[9,8,128]{2,1,0:T(8,128)S(1)}, u32[]{:S(2)}, u32[]{:S(2)}) collective-permute-start(f32[9,8,128]{2,1,0:T(8,128)S(1)} %get-tuple-element.17), channel_id=1, source_target_pairs={{128,0},{256,128},{384,256},{512,384},{640,512},{768,640},{896,768... | collective-permute-start | bytes 110600 | tf_op jit(solution)/shard_map/ppermute | solution.py:457
  3.7 3.1 %collective-permute-start = (f32[8,8,128]{2,1,0:T(8,128)S(1)}, f32[8,8,128]{2,1,0:T(8,128)S(1)}, u32[]{:S(2)}, u32[]{:S(2)}) collective-permute-start(f32[8,8,128]{2,1,0:T(8,128)S(1)} %get-tuple-element.16), channel_id=1, source_target_pairs={{0,128},{128,256},{256,384},{384,512},{512,640},{640,768},{768,896... | collective-permute-start | bytes 98312 | tf_op jit(solution)/shard_map/ppermute | solution.py:456
  6.9 1.1 %gather_block.1 = (f32[8,8,8,128]{3,2,1,0:T(8,128)S(1)}, s32[10,8,128]{2,1,0:T(8,128)S(1)}) custom-call(f32[8,8,128]{2,1,0:T(8,128)} %density.3, f32[3,8,8,128]{3,2,1,0:T(8,128)} %velocity.3, f32[8,8,128]{2,1,0:T(8,128)} %pressure.3, f32[3,8,8,128]{3,2,1,0:T(8,128)} %field.3, s32[64]{0:T(128)} %corona.1), custom_call_target="tpu_custom_call" | custom-call | tf_op jit(solution)/shard_map/gather_block/pallas_call | solution.py:458
  7.9 1.7 %collective-permute-done.below = f32[8,8,128]{2,1,0:T(8,128)S(1)} collective-permute-done((f32[8,8,128]{2,1,0:T(8,128)S(1)}, f32[8,8,128]{2,1,0:T(8,128)S(1)}, u32[]{:S(2)}, u32[]{:S(2)}) %collective-permute-start) | collective-permute-done | bytes 32800 | tf_op jit(solution)/shard_map/ppermute | solution.py:456
  9.6 0.0 collective-permute-done.1.above
  9.6 0.1 pack_rows.1
  9.7 17.7 %collective-permute-start.3 = (f32[96,128]{1,0:T(8,128)S(1)}, f32[96,128]{1,0:T(8,128)S(1)}, u32[]{:S(2)}, u32[]{:S(2)}) collective-permute-start(f32[96,128]{1,0:T(8,128)S(1)} %get-tuple-element.21), channel_id=1, source_target_pairs={{4,0},{8,4},{12,8},{16,12},{20,16},{24,20},{28,24},{32,28},{36,32}... | collective-permute-start | bytes 147464 | tf_op jit(solution)/shard_map/ppermute | solution.py:475
  27.4 1.9 %collective-permute-start.2 = (f32[88,128]{1,0:T(8,128)S(1)}, f32[88,128]{1,0:T(8,128)S(1)}, u32[]{:S(2)}, u32[]{:S(2)}) collective-permute-start(f32[88,128]{1,0:T(8,128)S(1)} %get-tuple-element.20), channel_id=1, source_target_pairs={{0,4},{4,8},{8,12},{12,16},{16,20},{20,24},{24,28},{28,32},{32,36}... | collective-permute-start | bytes 135176 | tf_op jit(solution)/shard_map/ppermute | solution.py:474
  29.3 0.3 pack_main.1
  29.6 4.7 %collective-permute-done.2.left_rows = f32[88,128]{1,0:T(8,128)S(1)} collective-permute-done((f32[88,128]{1,0:T(8,128)S(1)}, f32[88,128]{1,0:T(8,128)S(1)}, u32[]{:S(2)}, u32[]{:S(2)}) %collective-permute-start.2) | collective-permute-done | bytes 45088 | tf_op jit(solution)/shard_map/ppermute | solution.py:474
  34.3 0.0 collective-permute-done.3.right_rows
  34.3 0.5 pack_edges.1
  34.8 5.4 %collective-permute-start.4 = (f32[2,16,128]{2,1,0:T(8,128)S(1)}, f32[2,16,128]{2,1,0:T(8,128)S(1)}, u32[]{:S(2)}, u32[]{:S(2)}) collective-permute-start(f32[2,16,128]{2,1,0:T(8,128)S(1)} %get-tuple-element.22), channel_id=1, source_target_pairs={{0,1},{1,0},{2,3},{3,2},{4,5},{5,4},{6,7},{7,6},{8,9},{9,8},{10,11... | collective-permute-start | bytes 49160 | tf_op jit(solution)/shard_map/ppermute | solution.py:494
  40.2 3.0 %collective-permute-start.5 = (f32[2,16,128]{2,1,0:T(8,128)S(1)}, f32[2,16,128]{2,1,0:T(8,128)S(1)}, u32[]{:S(2)}, u32[]{:S(2)}) collective-permute-start(f32[2,16,128]{2,1,0:T(8,128)S(1)} %get-tuple-element.23), channel_id=1, source_target_pairs={{1,2},{2,1},{3,0},{0,3},{5,6},{6,5},{7,4},{4,7},{9,10},{10,9},{11,... | collective-permute-start | bytes 49160 | tf_op jit(solution)/shard_map/ppermute | solution.py:493
  43.2 0.0 collective-permute-done.4.near_in
  43.2 6.0 %collective-permute-done.5.far_in = f32[2,16,128]{2,1,0:T(8,128)S(1)} collective-permute-done((f32[2,16,128]{2,1,0:T(8,128)S(1)}, f32[2,16,128]{2,1,0:T(8,128)S(1)}, u32[]{:S(2)}, u32[]{:S(2)}) %collective-permute-start.5) | collective-permute-done | bytes 16416 | tf_op jit(solution)/shard_map/ppermute | solution.py:493
  49.2 2.2 %advance.1 = (f32[5,8,8,128]{3,2,1,0:T(8,128)}, f32[3,8,8,128]{3,2,1,0:T(8,128)}) custom-call(f32[2,16,128]{2,1,0:T(8,128)S(1)} %collective-permute-done.4.near_in, f32[2,16,128]{2,1,0:T(8,128)S(1)} %collective-permute-done.5.far_in, f32[3,16,128]{2,1,0:T(8,128)S(1)} %get-tuple-element.24.own_cols, f32[8,11,8,128]{3,2,1,0:T(8,128)S(1)} %get-tuple-element.18.main, ...), custom_call_target="tpu_custom_call" | custom-call | tf_op jit(solution)/shard_map/advance/pallas_call | solution.py:495
Async XLA Ops:
  1.6 8.0 %collective-permute-start.1 = (f32[9,8,128]{2,1,0:T(8,128)S(1)}, f32[9,8,128]{2,1,0:T(8,128)S(1)}, u32[]{:S(2)}, u32[]{:S(2)}) collective-permute-start(f32[9,8,128]{2,1,0:T(8,128)S(1)} %get-tuple-element.17), channel_id=1, source_target_pairs={{128,0},{256,128},{384,256},{512,384},{640,512},{768,640},{896,768... | collective-permute-start | bytes 110600 | tf_op jit(solution)/shard_map/ppermute | solution.py:457
  3.7 5.9 %collective-permute-start = (f32[8,8,128]{2,1,0:T(8,128)S(1)}, f32[8,8,128]{2,1,0:T(8,128)S(1)}, u32[]{:S(2)}, u32[]{:S(2)}) collective-permute-start(f32[8,8,128]{2,1,0:T(8,128)S(1)} %get-tuple-element.16), channel_id=1, source_target_pairs={{0,128},{128,256},{256,384},{384,512},{512,640},{640,768},{768,896... | collective-permute-start | bytes 98312 | tf_op jit(solution)/shard_map/ppermute | solution.py:456
  9.7 24.6 %collective-permute-start.3 = (f32[96,128]{1,0:T(8,128)S(1)}, f32[96,128]{1,0:T(8,128)S(1)}, u32[]{:S(2)}, u32[]{:S(2)}) collective-permute-start(f32[96,128]{1,0:T(8,128)S(1)} %get-tuple-element.21), channel_id=1, source_target_pairs={{4,0},{8,4},{12,8},{16,12},{20,16},{24,20},{28,24},{32,28},{36,32}... | collective-permute-start | bytes 147464 | tf_op jit(solution)/shard_map/ppermute | solution.py:475
  27.4 6.9 %collective-permute-start.2 = (f32[88,128]{1,0:T(8,128)S(1)}, f32[88,128]{1,0:T(8,128)S(1)}, u32[]{:S(2)}, u32[]{:S(2)}) collective-permute-start(f32[88,128]{1,0:T(8,128)S(1)} %get-tuple-element.20), channel_id=1, source_target_pairs={{0,4},{4,8},{8,12},{12,16},{16,20},{20,24},{24,28},{28,32},{32,36}... | collective-permute-start | bytes 135176 | tf_op jit(solution)/shard_map/ppermute | solution.py:474
  34.8 8.4 %collective-permute-start.4 = (f32[2,16,128]{2,1,0:T(8,128)S(1)}, f32[2,16,128]{2,1,0:T(8,128)S(1)}, u32[]{:S(2)}, u32[]{:S(2)}) collective-permute-start(f32[2,16,128]{2,1,0:T(8,128)S(1)} %get-tuple-element.22), channel_id=1, source_target_pairs={{0,1},{1,0},{2,3},{3,2},{4,5},{5,4},{6,7},{7,6},{8,9},{9,8},{10,11... | collective-permute-start | bytes 49160 | tf_op jit(solution)/shard_map/ppermute | solution.py:494
  40.2 9.0 %collective-permute-start.5 = (f32[2,16,128]{2,1,0:T(8,128)S(1)}, f32[2,16,128]{2,1,0:T(8,128)S(1)}, u32[]{:S(2)}, u32[]{:S(2)}) collective-permute-start(f32[2,16,128]{2,1,0:T(8,128)S(1)} %get-tuple-element.23), channel_id=1, source_target_pairs={{1,2},{2,1},{3,0},{0,3},{5,6},{6,5},{7,4},{4,7},{9,10},{10,9},{11,... | collective-permute-start | bytes 49160 | tf_op jit(solution)/shard_map/ppermute | solution.py:493
